TPU v7x, 32 devices: a 4x4x1 block of a 4x4x8 slice. The times are simulated.
32 devices in a mesh: rep: 1 (over z), r: 4 (over y), s: 8 (over x, core).
Axes of the slice: x: 4, y: 4, z: 1, core: 2. Of those that a mesh axis runs over, the one named last changes fastest.
The devices are a block of a 4x4x8 slice.
Arguments:
- x: bfloat16 [32, 2048, 1024], P(('rep', 'r', 's'))
- dy: bfloat16 [32, 2048, 1024], P(('rep', 'r', 's'))
- w_gate: bfloat16 [2, 1024, 2816], P(None, 's')
- w_up: bfloat16 [2, 1024, 2816], P(None, 's')
- w_down: bfloat16 [2, 2816, 1024], P(None, 's')
- m_w_gate: float32 [2, 1024, 2816], P(None, 's')
- m_w_up: float32 [2, 1024, 2816], P(None, 's')
- m_w_down: float32 [2, 2816, 1024], P(None, 's')
- v_w_gate: float32 [2, 1024, 2816], P(None, 's')
- v_w_up: float32 [2, 1024, 2816], P(None, 's')
- v_w_down: float32 [2, 2816, 1024], P(None, 's')
Outputs:
- output 1: bfloat16 [2, 1024, 2816], P('rep', 's')
- output 2: bfloat16 [2, 1024, 2816], P('rep', 's')
- output 3: bfloat16 [2, 2816, 1024], P('rep', 's')
- output 4: float32 [2, 1024, 2816], P('rep', 's')
- output 5: float32 [2, 1024, 2816], P('rep', 's')
- output 6: float32 [2, 2816, 1024], P('rep', 's')
- output 7: float32 [2, 1024, 2816], P('rep', 's')
- output 8: float32 [2, 1024, 2816], P('rep', 's')
- output 9: float32 [2, 2816, 1024], P('rep', 's')
All inputs are finite; a program needn't handle non-finite values.
Results may differ from a plain program's by a relative error of at most 0.02.
Values are sent between devices in bfloat16 or wider.
A program may use at most 768 MiB of HBM per device.

v0:
```python
import jax
import jax.numpy as jnp
from jax import lax
from jax.sharding import PartitionSpec as P

NAMES = ("w_gate", "w_up", "w_down")


def matmul(a, w):
    return jnp.dot(a, w, preferred_element_type=jnp.float32).astype(jnp.bfloat16)


def normed(h):
    wide = h.astype(jnp.float32)
    scale = lax.rsqrt(jnp.mean(wide**2, -1, keepdims=True) + 1e-6)
    return (wide * scale).astype(jnp.bfloat16)


def layer(h, w):
    a = normed(h)
    gate = jnp.dot(a, w["w_gate"], preferred_element_type=jnp.float32)
    up = jnp.dot(a, w["w_up"], preferred_element_type=jnp.float32)
    return h + matmul((jax.nn.silu(gate) * up).astype(jnp.bfloat16), w["w_down"])


def adamw(w, m, v, g):
    m = 0.9 * m + 0.1 * g
    v = 0.95 * v + 0.05 * g * g
    step = m * lax.rsqrt(v + 1e-8) + 0.1 * w
    return (w - 0.02 * step).astype(jnp.bfloat16), m, v


def solution(mesh):
    def fetched(weights, number):
        return {name: lax.all_gather(w[number], "s", axis=0, tiled=True) for name, w in zip(NAMES, weights, strict=True)}

    def summed(term):
        return lax.psum(lax.psum_scatter(term, "s", scatter_dimension=0, tiled=True), "r")

    def step(x, dy, *arrays):
        weights, m, v = (arrays[i : i + 3] for i in (0, 3, 6))
        layers = weights[0].shape[0]
        h, kept = x[0], []
        for number in range(layers):
            kept.append(h)
            h = layer(h, fetched(weights, number))
        by_h, mine = dy[0], [None] * layers
        for number in reversed(range(layers)):
            _, back = jax.vjp(lambda w, h: layer(h, w), fetched(weights, number), kept[number])
            by_w, by_h = back(by_h)
            mine[number] = [summed(by_w[name]) for name in NAMES]
        gradients = [jnp.stack([mine[number][i] for number in range(layers)]).astype(jnp.float32) for i in range(3)]
        new = [adamw(w.astype(jnp.float32), m, v, g) for w, m, v, g in zip(weights, m, v, gradients, strict=True)]
        return tuple(one[which] for which in range(3) for one in new)

    states, cut = P(("rep", "r", "s"), None, None), P(None, "s", None)
    return jax.shard_map(
        step,
        mesh=mesh,
        in_specs=(states, states) + (cut,) * 9,
        out_specs=(P("rep", "s", None),) * 9,
        check_vma=False,
    )
```

profile of v0, /device:TPU:97, one launch (start us, length us, event | category | flops | bytes accessed | tf_op | source)
XLA Modules:
  0.0 696.0 jit_solution(13205991866199955157)
XLA Ops:
  7.2 0.1 all-gather.13.cloned.1.call-start
  7.3 2.6 fusion.88
  9.9 0.1 all-gather.13.cloned.1.call-update
  9.9 0.1 all-gather.15.cloned.1.call-start
  10.0 2.5 fusion.87
  12.5 0.1 all-gather.15.cloned.1.call-update
  12.6 0.1 all-gather.17.cloned.1.call-start
  12.7 1.2 fusion.86
  13.9 0.1 all-gather.17.cloned.1.call-update
  13.9 0.1 all-gather.21.cloned.1.call-start
  14.0 0.6 all-gather.21.cloned.1.call-update
  14.6 0.1 all-gather.23.cloned.1.call-start
  14.7 0.6 all-gather.23.cloned.1.call-update
  15.2 0.1 all-gather.19.cloned.1.call-start
  15.3 0.6 all-gather.19.cloned.1.call-update
  15.9 0.1 reduce-scatter.15.cloned.1.call-start
  15.9 6.5 copy.20
  22.4 3.1 fusion.15
  25.5 6.5 copy.21
  32.0 18.4 %all-gather.13.cloned.1.call-done = bf16[1,1024,2816]{2,1,0:T(8,128)(2,1)} async-done(((bf16[1,128,2816]{2,1,0:T(8,128)(2,1)}), bf16[1,1024,2816]{2,1,0:T(8,128)(2,1)}) %all-gather.13.cloned.1.call-update) | async-done | bytes 5767184 | tf_op jit(solution)/shard_map/all_gather | solution.py:35
  50.4 19.9 %fusion.35 = f32[2048,2816]{1,0:T(8,128)} fusion(bf16[1,1024,2816]{2,1,0:T(8,128)(2,1)} %all-gather.13.cloned.1.call-done, bf16[1,2048,1024]{1,2,0:T(8,128)(2,1)} %copy.20, f32[2048]{0:T(1024)S(1)} %add_rsqrt_fusion), kind=kOutput, calls=%fused_computation.53 | convolution fusion | flops 11817451520 | bytes 33038336 | tf_op jit(solution)/shard_map/dot_general | solution.py:21
  70.3 18.2 %all-gather.15.cloned.1.call-done = bf16[1,1024,2816]{2,1,0:T(8,128)(2,1)} async-done(((bf16[1,128,2816]{2,1,0:T(8,128)(2,1)}), bf16[1,1024,2816]{2,1,0:T(8,128)(2,1)}) %all-gather.15.cloned.1.call-update) | async-done | bytes 5767184 | tf_op jit(solution)/shard_map/all_gather | solution.py:35
  88.5 27.8 %multiply_convert_fusion.1 = (bf16[2048,2816]{1,0:T(8,128)(2,1)}, f32[2048,2816]{1,0:T(8,128)}) fusion(f32[2048,2816]{1,0:T(8,128)} %fusion.35, bf16[1,1024,2816]{2,1,0:T(8,128)(2,1)} %all-gather.15.cloned.1.call-done, bf16[1,2048,1024]{1,2,0:T(8,128)(2,1)} %copy.20, f32[2048]{0:T(1024)S(1)} %add_rsqrt_fusion), kind=kOutput, calls=%fused_computation.17 | convolution fusion | flops 11852054528 | bytes 67641344 | tf_op jit(solution)/shard_map/dot_general | solution.py:22
  116.3 10.3 %all-gather.17.cloned.1.call-done = bf16[1,2816,1024]{2,1,0:T(8,128)(2,1)} async-done(((bf16[1,352,1024]{2,1,0:T(8,128)(2,1)}), bf16[1,2816,1024]{2,1,0:T(8,128)(2,1)}) %all-gather.17.cloned.1.call-update) | async-done | bytes 5767184 | tf_op jit(solution)/shard_map/all_gather | solution.py:35
  126.6 19.8 %fusion.19 = (f32[2048]{0:T(1024)S(1)}, bf16[2048,1024]{0,1:T(8,128)(2,1)}) fusion(bf16[2048,2816]{1,0:T(8,128)(2,1)} %get-tuple-element.30, bf16[1,2816,1024]{2,1,0:T(8,128)(2,1)} %all-gather.17.cloned.1.call-done, bf16[1,2048,1024]{1,2,0:T(8,128)(2,1)} %copy.20), kind=kOutput, calls=%fused_computation.37 | convolution fusion | flops 11821643776 | bytes 25698304 | tf_op jit(solution)/shard_map/dot_general | solution.py:10
  146.4 18.2 %all-gather.21.cloned.1.call-done = bf16[1,2816,1024]{2,1,0:T(8,128)(2,1)} async-done(((bf16[1,352,1024]{2,1,0:T(8,128)(2,1)}), bf16[1,2816,1024]{2,1,0:T(8,128)(2,1)}) %all-gather.21.cloned.1.call-update) | async-done | bytes 5767184 | tf_op jit(solution)/shard_map/all_gather | solution.py:35
  164.6 18.1 %convolution_convert_fusion.1 = bf16[2048,2816]{1,0:T(8,128)(2,1)} fusion(bf16[1,2816,1024]{2,1,0:T(8,128)(2,1)} %all-gather.21.cloned.1.call-done, bf16[1,2048,1024]{2,1,0:T(8,128)(2,1)} %param.12), kind=kOutput, calls=%fused_computation.29 | convolution fusion | flops 11816927232 | bytes 21495808 | tf_op jit(solution)/shard_map/transpose(jvp())/dot_general | solution.py:10
  182.8 19.9 %all-gather.23.cloned.1.call-done = bf16[1,1024,2816]{2,1,0:T(8,128)(2,1)} async-done(((bf16[1,128,2816]{2,1,0:T(8,128)(2,1)}), bf16[1,1024,2816]{2,1,0:T(8,128)(2,1)}) %all-gather.23.cloned.1.call-update) | async-done | bytes 5767184 | tf_op jit(solution)/shard_map/all_gather | solution.py:35
  202.6 20.1 %fusion.22 = f32[2048,2816]{1,0:T(8,128)} fusion(bf16[1,1024,2816]{2,1,0:T(8,128)(2,1)} %all-gather.23.cloned.1.call-done, bf16[2048,1024]{0,1:T(8,128)(2,1)} %get-tuple-element.33, f32[2048]{0:T(1024)S(1)} %fusion.74), kind=kOutput, calls=%fused_computation.40 | convolution fusion | flops 11817451520 | bytes 33038336 | tf_op jit(solution)/shard_map/jvp()/dot_general | solution.py:22
  222.7 17.9 %all-gather.19.cloned.1.call-done = bf16[1,1024,2816]{2,1,0:T(8,128)(2,1)} async-done(((bf16[1,128,2816]{2,1,0:T(8,128)(2,1)}), bf16[1,1024,2816]{2,1,0:T(8,128)(2,1)}) %all-gather.19.cloned.1.call-update) | async-done | bytes 5767184 | tf_op jit(solution)/shard_map/all_gather | solution.py:35
  240.6 34.4 %fusion.2 = (bf16[2048,2816]{1,0:T(8,128)(2,1)}, f32[2048,2816]{1,0:T(8,128)}) fusion(f32[2048,2816]{1,0:T(8,128)} %fusion.22, bf16[2048,2816]{1,0:T(8,128)(2,1)} %convolution_convert_fusion.1, bf16[1,1024,2816]{2,1,0:T(8,128)(2,1)} %all-gather.19.cloned.1.call-done, bf16[2048,1024]{0,1:T(8,128)(2,1)} %get-tuple-element.33, f32[2048]{0:T(1024)S(1)} %fusion.74), kind=kOutput, calls=%fused_computation.8 | convolution fusion | flops 11886657536 | bytes 79175680 | tf_op jit(solution)/shard_map/jvp()/dot_general | solution.py:21
  275.0 21.7 %fusion.12 = bf16[2048,1024]{0,1:T(8,128)(2,1)} fusion(bf16[2048,2816]{1,0:T(8,128)(2,1)} %convolution_convert_fusion.1, bf16[1,1024,2816]{2,1,0:T(8,128)(2,1)} %all-gather.23.cloned.1.call-done, f32[2048,2816]{1,0:T(8,128)} %get-tuple-element.35), kind=kOutput, calls=%fused_computation.21 | convolution fusion | flops 11845763072 | bytes 44564480 | tf_op jit(solution)/shard_map/transpose(jvp())/dot_general | solution.py:22
  296.7 18.9 %fusion.21 = (f32[2048]{0:T(1024)S(1)}, bf16[2048,1024]{0,1:T(8,128)(2,1)S(1)}) fusion(bf16[2048,1024]{0,1:T(8,128)(2,1)} %get-tuple-element.33, bf16[2048,1024]{0,1:T(8,128)(2,1)} %fusion.12, bf16[2048,2816]{1,0:T(8,128)(2,1)} %get-tuple-element.34, bf16[1,1024,2816]{2,1,0:T(8,128)(2,1)} %all-gather.19.cloned.1.call-done), kind=kOutput, calls=%fused_computation.39 | convolution fusion | flops 11821643776 | bytes 29892608 | tf_op jit(solution)/shard_map/transpose(jvp())/dot_general | solution.py:21
  315.7 3.6 fusion.43
  319.3 2.0 copy-done.6
  321.3 17.2 %convolution_convert_fusion.2 = bf16[2816,1024]{1,0:T(8,128)(2,1)} fusion(bf16[2048,2816]{1,0:T(8,128)(2,1)} %get-tuple-element.30, bf16[2048,1024]{0,1:T(8,128)(2,1)S(1)} %fusion.43), kind=kOutput, calls=%fused_computation.59 | convolution fusion | flops 11814043648 | bytes 21495808 | tf_op jit(solution)/shard_map/transpose(jvp())/dot_general | solution.py:10
  338.4 0.1 reduce-scatter.15.cloned.1.call-update
  338.5 0.1 reduce-scatter.17.cloned.1.call-start
  338.6 23.6 %fusion.37 = bf16[2816,1024]{1,0:T(8,128)(2,1)} fusion(f32[2048,2816]{1,0:T(8,128)} %fusion.22, bf16[1,2048,1024]{2,1,0:T(8,128)(2,1)} %param.12, f32[2048,2816]{1,0:T(8,128)} %get-tuple-element.35), kind=kOutput, calls=%fused_computation.55 | convolution fusion | flops 11848646656 | bytes 56098816 | tf_op jit(solution)/shard_map/transpose(jvp())/dot_general | solution.py:10
  362.2 0.1 reduce-scatter.17.cloned.1.call-update
  362.3 0.1 reduce-scatter.11.cloned.1.call-start
  362.3 18.5 %convolution_convert_fusion = bf16[2048,2816]{1,0:T(8,128)(2,1)} fusion(bf16[2048,1024]{0,1:T(8,128)(2,1)} %copy-done.6, bf16[1,2816,1024]{2,1,0:T(8,128)(2,1)} %all-gather.17.cloned.1.call-done), kind=kOutput, calls=%fused_computation.28 | convolution fusion | flops 11816927232 | bytes 21495808 | tf_op jit(solution)/shard_map/transpose(jvp())/dot_general | solution.py:10
  380.8 22.5 %fusion.42 = bf16[1024,2816]{1,0:T(8,128)(2,1)} fusion(bf16[2048,2816]{1,0:T(8,128)(2,1)} %convolution_convert_fusion, f32[2048,2816]{1,0:T(8,128)} %fusion.35, bf16[1,2048,1024]{1,2,0:T(8,128)(2,1)} %copy.20, f32[2048]{0:T(1024)S(1)} %copy-done.18), kind=kOutput, calls=%fused_computation.58 | convolution fusion | flops 11854938112 | bytes 44572672 | tf_op jit(solution)/shard_map/transpose(jvp())/dot_general | solution.py:22
  403.3 0.1 reduce-scatter.11.cloned.1.call-update
  403.4 0.1 reduce-scatter.13.cloned.1.call-start
  403.4 0.6 copy-done.14
  404.0 22.6 %fusion.38 = bf16[1024,2816]{1,0:T(8,128)(2,1)} fusion(bf16[2048,2816]{1,0:T(8,128)(2,1)} %convolution_convert_fusion.1, bf16[2048,1024]{0,1:T(8,128)(2,1)} %get-tuple-element.33, f32[2048]{0:T(1024)S(1)} %copy-done.14, f32[2048,2816]{1,0:T(8,128)} %get-tuple-element.35), kind=kOutput, calls=%fused_computation.56 | convolution fusion | flops 11854938112 | bytes 44572672 | tf_op jit(solution)/shard_map/transpose(jvp())/dot_general | solution.py:22
  426.6 0.1 reduce-scatter.13.cloned.1.call-update
  426.7 0.1 reduce-scatter.7.cloned.1.call-start
  426.7 27.3 %fusion.39 = bf16[1024,2816]{1,0:T(8,128)(2,1)} fusion(f32[2048,2816]{1,0:T(8,128)} %fusion.35, f32[2048,2816]{1,0:T(8,128)} %get-tuple-element.31, bf16[2048,2816]{1,0:T(8,128)(2,1)} %convolution_convert_fusion, bf16[1,2048,1024]{1,2,0:T(8,128)(2,1)} %copy.20, f32[2048]{0:T(1024)S(1)} %copy-done.18), kind=kOutput, calls=%fused_computation.57 | convolution fusion | flops 11883773952 | bytes 67641344 | tf_op jit(solution)/shard_map/transpose(jvp())/dot_general | solution.py:21
  454.1 0.1 reduce-scatter.9.cloned.1.call-start
  454.2 18.9 %convolution_convert_fusion.3 = bf16[1024,2816]{1,0:T(8,128)(2,1)} fusion(bf16[2048,2816]{1,0:T(8,128)(2,1)} %get-tuple-element.34, bf16[2048,1024]{0,1:T(8,128)(2,1)} %get-tuple-element.33, f32[2048]{0:T(1024)S(1)} %copy-done.14), kind=kOutput, calls=%fused_computation.60 | convolution fusion | flops 11817451520 | bytes 21504000 | tf_op jit(solution)/shard_map/transpose(jvp())/dot_general | solution.py:21
  473.1 0.1 all-reduce.3.cloned.1.call-start
  473.3 23.5 %reduce-scatter.13.cloned.1.call-done = bf16[128,2816]{1,0:T(8,128)(2,1)} async-done(((bf16[1024,2816]{1,0:T(8,128)(2,1)}), bf16[128,2816]{1,0:T(8,128)(2,1)}) %reduce-scatter.13.cloned.1.call-update) | async-done | bytes 720912 | tf_op jit(solution)/shard_map/reduce_scatter | solution.py:38
  496.8 40.5 %reduce-scatter.7.cloned.1.call-done = bf16[128,2816]{1,0:T(8,128)(2,1)} async-done(((bf16[1024,2816]{1,0:T(8,128)(2,1)}), bf16[128,2816]{1,0:T(8,128)(2,1)}) %reduce-scatter.7.cloned.1.call-update) | async-done | bytes 720912 | tf_op jit(solution)/shard_map/reduce_scatter | solution.py:38
  537.3 40.3 %reduce-scatter.9.cloned.1.call-done = bf16[128,2816]{1,0:T(8,128)(2,1)} async-done(((bf16[1024,2816]{1,0:T(8,128)(2,1)}), bf16[128,2816]{1,0:T(8,128)(2,1)}) %reduce-scatter.9.cloned.1.call-update) | async-done | bytes 720912 | tf_op jit(solution)/shard_map/reduce_scatter | solution.py:38
  577.7 93.4 %all-reduce.3.cloned.1.call-done = (bf16[1,128,2816]{2,1,0:T(8,128)(2,1)}, bf16[1,128,2816]{2,1,0:T(8,128)(2,1)}, bf16[1,128,2816]{2,1,0:T(8,128)(2,1)}, bf16[1,...) async-done(((bf16[1,128,2816]{2,1,0:T(8,128)(2,1)}, bf16[1,128,2816]{2,1,0:T(8,128)(2,1)}, bf16[1,128,2816]{2,1,0:T(8,128)(2,1)}, ...) | async-done | bytes 4325392 | tf_op jit(solution)/shard_map/psum | solution.py:38
  671.1 6.6 fusion.61
  677.8 1.5 copy-done.8
  679.3 0.8 copy-done.9
  680.1 0.8 copy-done.10
  680.9 0.1 copy-done.11
  681.0 0.2 copy-done.12
  681.2 7.8 %fusion.53 = (bf16[2,128,2816]{2,1,0:T(8,128)(2,1)}, f32[2,128,2816]{2,1,0:T(8,128)}, f32[2,128,2816]{2,1,0:T(8,128)}, bf16[2,128,2816]{2,1,0:T(8,128)(2,1)}, f3...) fusion(bf16[2,128,2816]{2,1,0:T(8,128)(2,1)S(1)} %copy-done.1, bf16[1,128,2816]{2,1,0:T(8,128)(2,1)S(1)} %copy-done.11, ...), kind=kLoop, calls=%fused_computation.80 | loop fusion | flops 27394048 | bytes 31719424 | tf_op jit(solution)/shard_map/convert_element_type | solution.py:30
  (40 shorter events, 0.3 us)
Async XLA Ops:
  7.2 5.5 copy-start.3
  7.2 43.2 %all-gather.13.cloned.1.call-start = ((), (), s32[]{:S(2)}) async-start(), calls=%async_computation.12 | async-start | bytes 6488064 | tf_op jit(solution)/shard_map/all_gather | solution.py:35
  9.9 78.6 %all-gather.15.cloned.1.call-start = ((), (), s32[]{:S(2)}) async-start(), calls=%async_computation.13 | async-start | bytes 6488064 | tf_op jit(solution)/shard_map/all_gather | solution.py:35
  12.6 114.0 %all-gather.17.cloned.1.call-start = ((), (), s32[]{:S(2)}) async-start(), calls=%async_computation.14 | async-start | bytes 6488064 | tf_op jit(solution)/shard_map/all_gather | solution.py:35
  13.9 150.7 %all-gather.21.cloned.1.call-start = ((), (), s32[]{:S(2)}) async-start(), calls=%async_computation.16 | async-start | bytes 6488064 | tf_op jit(solution)/shard_map/all_gather | solution.py:35
  14.6 188.0 %all-gather.23.cloned.1.call-start = ((), (), s32[]{:S(2)}) async-start(), calls=%async_computation.17 | async-start | bytes 6488064 | tf_op jit(solution)/shard_map/all_gather | solution.py:35
  15.2 225.4 %all-gather.19.cloned.1.call-start = ((), (), s32[]{:S(2)}) async-start(), calls=%async_computation.15 | async-start | bytes 6488064 | tf_op jit(solution)/shard_map/all_gather | solution.py:35
  15.9 457.3 %reduce-scatter.15.cloned.1.call-start = ((), (), s32[]{:S(2)}) async-start(), calls=%async_computation.10 | async-start | bytes 6488064 | tf_op jit(solution)/shard_map/reduce_scatter | solution.py:38
  25.5 63.0 %copy-start.17 = (f32[2048]{0:T(1024)}, f32[2048]{0:T(1024)S(1)}, u32[]{:S(2)}) copy-start(f32[2048]{0:T(1024)S(1)} %add_rsqrt_fusion) | copy-start | bytes 24580
  146.4 36.4 %copy-start.15 = (f32[2048]{0:T(1024)}, f32[2048]{0:T(1024)S(1)}, u32[]{:S(2)}) copy-start(f32[2048]{0:T(1024)S(1)} %get-tuple-element.32) | copy-start | bytes 24580
  146.4 169.2 %copy-start.13 = (f32[2048]{0:T(1024)}, f32[2048]{0:T(1024)S(1)}, u32[]{:S(2)}) copy-start(f32[2048]{0:T(1024)S(1)} %fusion.74) | copy-start | bytes 24580
  296.7 18.9 %copy-start.16 = (f32[2048]{0:T(1024)S(1)}, f32[2048]{0:T(1024)}, u32[]{:S(2)}) copy-start(f32[2048]{0:T(1024)} %copy-done.15) | copy-start | bytes 24580
  296.7 18.9 %copy-start = (bf16[1,2048,1024]{1,2,0:T(8,128)(2,1)S(1)}, bf16[1,2048,1024]{1,2,0:T(8,128)(2,1)}, u32[]{:S(2)}) copy-start(bf16[1,2048,1024]{1,2,0:T(8,128)(2,1)} %copy.21) | copy-start | bytes 12582916
  296.7 18.9 %copy-start.5 = (bf16[2048,1024]{0,1:T(8,128)(2,1)S(1)}, bf16[2048,1024]{0,1:T(8,128)(2,1)}, u32[]{:S(2)}) copy-start(bf16[2048,1024]{0,1:T(8,128)(2,1)} %get-tuple-element.33) | copy-start | bytes 12582916
  319.3 2.0 copy-start.6
  338.5 134.7 %reduce-scatter.17.cloned.1.call-start = ((), (), s32[]{:S(2)}) async-start(), calls=%async_computation.11 | async-start | bytes 6488064 | tf_op jit(solution)/shard_map/reduce_scatter | solution.py:38
  362.3 18.6 %copy-start.18 = (f32[2048]{0:T(1024)S(1)}, f32[2048]{0:T(1024)}, u32[]{:S(2)}) copy-start(f32[2048]{0:T(1024)} %copy-done.17) | copy-start | bytes 24580
  362.3 111.0 %reduce-scatter.11.cloned.1.call-start = ((), (), s32[]{:S(2)}) async-start(), calls=%async_computation.8 | async-start | bytes 6488064 | tf_op jit(solution)/shard_map/reduce_scatter | solution.py:38
  403.3 0.7 copy-start.14
  403.4 93.4 %reduce-scatter.13.cloned.1.call-start = ((), (), s32[]{:S(2)}) async-start(), calls=%async_computation.9 | async-start | bytes 6488064 | tf_op jit(solution)/shard_map/reduce_scatter | solution.py:38
  426.7 110.6 %reduce-scatter.7.cloned.1.call-start = ((), (), s32[]{:S(2)}) async-start(), calls=%async_computation.6 | async-start | bytes 6488064 | tf_op jit(solution)/shard_map/reduce_scatter | solution.py:38
  454.1 123.5 %reduce-scatter.9.cloned.1.call-start = ((), (), s32[]{:S(2)}) async-start(), calls=%async_computation.7 | async-start | bytes 6488064 | tf_op jit(solution)/shard_map/reduce_scatter | solution.py:38
  473.0 198.0 %copy-start.4 = (bf16[2,352,1024]{2,1,0:T(8,128)(2,1)S(1)}, bf16[2,352,1024]{2,1,0:T(8,128)(2,1)}, u32[]{:S(2)}) copy-start(bf16[2,352,1024]{2,1,0:T(8,128)(2,1)} %param.15) | copy-start | bytes 4325380
  473.1 198.0 %all-reduce.3.cloned.1.call-start = ((), (), s32[]{:S(2)}) async-start(), calls=%async_computation.18 | async-start | bytes 8650752 | tf_op jit(solution)/shard_map/psum | solution.py:38
  671.1 6.7 copy-start.1
  671.1 6.7 copy-start.2
  671.1 6.7 copy-start.7
  671.1 8.2 %copy-start.8 = (f32[2,128,2816]{2,1,0:T(8,128)S(1)}, f32[2,128,2816]{2,1,0:T(8,128)}, u32[]{:S(2)}) copy-start(f32[2,128,2816]{2,1,0:T(8,128)} %param.16) | copy-start | bytes 8650756
  671.1 9.0 %copy-start.9 = (f32[2,128,2816]{2,1,0:T(8,128)S(1)}, f32[2,128,2816]{2,1,0:T(8,128)}, u32[]{:S(2)}) copy-start(f32[2,128,2816]{2,1,0:T(8,128)} %param.20) | copy-start | bytes 8650756
  671.1 9.8 %copy-start.10 = (f32[2,128,2816]{2,1,0:T(8,128)S(1)}, f32[2,128,2816]{2,1,0:T(8,128)}, u32[]{:S(2)}) copy-start(f32[2,128,2816]{2,1,0:T(8,128)} %param.17) | copy-start | bytes 8650756
  671.1 9.9 %copy-start.11 = (bf16[1,128,2816]{2,1,0:T(8,128)(2,1)S(1)}, bf16[1,128,2816]{2,1,0:T(8,128)(2,1)}, u32[]{:S(2)}) copy-start(bf16[1,128,2816]{2,1,0:T(8,128)(2,1)} %get-tuple-element.9) | copy-start | bytes 2162692
  671.1 10.1 %copy-start.12 = (bf16[1,128,2816]{2,1,0:T(8,128)(2,1)S(1)}, bf16[1,128,2816]{2,1,0:T(8,128)(2,1)}, u32[]{:S(2)}) copy-start(bf16[1,128,2816]{2,1,0:T(8,128)(2,1)} %get-tuple-element.10) | copy-start | bytes 2162692
Sparse Core Ops, SparseCore 0:
  10.2 40.1 all-gather.12
  52.5 35.9 all-gather.14
  90.7 35.9 all-gather.16
  128.7 35.9 all-gather.20
  166.7 35.9 all-gather.22
  204.7 35.9 all-gather.18
  338.6 36.7 reduce-scatter.14
  377.7 38.1 reduce-scatter.16
  418.2 38.1 reduce-scatter.10
  458.6 38.1 reduce-scatter.12
  499.1 38.1 reduce-scatter.6
  539.4 38.1 reduce-scatter.8
  580.4 90.6 all-reduce.2
where the time goes:
time: 705 us; the launch traced here: 696 us
  matrix products  331 us (47%)
  waiting for transfers between devices  303 us (43%)
  local copies, waits for them, and re-layouts  25.4 us (4%)
  other arithmetic  21.1 us (3%)
  between operations  14.6 us (2%)
    dot_general x5, matrix products, layer(): gate = jnp.dot(a, w['w_gate'], preferred_element_type=jnp.float32)  119 us
    dot_general x5, matrix products, layer(): up = jnp.dot(a, w['w_up'], preferred_element_type=jnp.float32)  115 us
    reduce_scatter x6, waiting for transfers between devices, summed(): lax.psum_scatter(term, 's', scatter_dimension=0, tiled=True)  104 us
    all_gather x6, waiting for transfers between devices, fetched(): lax.all_gather(w[number], 's', axis=0, tiled=True)  103 us
    dot_general x5, matrix products, matmul(): jnp.dot(a, w, preferred_element_type=jnp.float32).astype(jnp.bfloat16)  97.2 us
    psum x1, waiting for transfers between devices, summed(): lax.psum(lax.psum_scatter(term, 's', scatter_dimension=0, tiled=True), 'r')  93.4 us
    unnamed x40, local copies, waits for them, and re-layouts  19.1 us
    convert_element_type x2, other arithmetic, adamw(): return ((w - 0.02 * step).astype(jnp.bfloat16), m, v)  14.4 us
  transfers between devices with their start and end apart: 13, of which 10 were waited for; matrix products, arithmetic and copies ran while one was open for 37% of the time, Pallas kernels for 0%

commit v1 on v0

v1 whole, which is shorter than its diff:
```python
import jax
import jax.numpy as jnp
from jax import lax
from jax.experimental import pallas as pl
from jax.experimental.pallas import tpu as pltpu
from jax.sharding import PartitionSpec as P

NAMES = ("w_gate", "w_up", "w_down")
BF, F32 = jnp.bfloat16, jnp.float32
NN, NT, TN = ((((1,), (0,)), ((), ())), (((1,), (1,)), ((), ())), (((0,), (0,)), ((), ())))
MESH = pl.DeviceIdType.MESH
BN = 256


def mm(a, b, dims=NN):
    return lax.dot_general(a, b, dims, preferred_element_type=F32)


def whole(shape):
    return pl.BlockSpec(shape, lambda j: (0,) * len(shape), pipeline_mode=pl.Buffered(1))


def cols(rows, n):
    return pl.BlockSpec((rows, n), lambda j: (0, j))


def rows(m, columns):
    return pl.BlockSpec((m, columns), lambda j: (j, 0))


def sds(shape, dtype=BF):
    return jax.ShapeDtypeStruct(shape, dtype)


def normed(wide):
    return (wide * lax.rsqrt(jnp.mean(wide * wide, -1, keepdims=True) + 1e-6)).astype(BF)


class Place:
    def __init__(self, mesh):
        self.nx, self.ny = mesh.shape["s"] // 2, mesh.shape["r"]
        s = lax.axis_index("s")
        self.x, self.c, self.y = s // 2, s % 2, lax.axis_index("r")
        self.to = {
            "x+": {"s": (s + 2) % (2 * self.nx)},
            "x-": {"s": (s + 2 * self.nx - 2) % (2 * self.nx)},
            "y+": {"r": (self.y + 1) % self.ny},
            "y-": {"r": (self.y + self.ny - 1) % self.ny},
            "d": {"s": s + 1 - 2 * self.c},
        }

    def meet(self):
        barrier = pltpu.get_barrier_semaphore()
        for target in self.to.values():
            pl.semaphore_signal(barrier, inc=1, device_id=target, device_id_type=MESH)
        pl.semaphore_wait(barrier, len(self.to))


class Gather:
    def __init__(self, place, by, shard, full, stage, send, recv, local):
        self.p, self.by, self.shard, self.full, self.stage = place, by, shard, full, stage
        self.send, self.recv, self.local = send, recv, local
        self.n = shard.shape[0]
        self.stages = 3 if by == "x" else 5

    def span(self, x, start=0, size=None):
        p = self.p
        return pl.ds(pl.multiple_of((2 * (x % p.nx) + p.c) * self.n + start, 8), self.n if size is None else size)

    def copy(self, k, way, x, start=0, size=None, own=False):
        at = self.full.at[self.span(x, start, size)]
        src = at
        if own:
            src = self.shard.at[pl.ds(pl.multiple_of(start, 8) if size else 0, size or self.n)]
        return lambda: pltpu.make_async_remote_copy(
            src_ref=src, dst_ref=at, send_sem=self.send.at[k], recv_sem=self.recv.at[k], device_id=self.p.to[way], device_id_type=MESH
        )

    def copies(self):
        p, n, x = self.p, self.n, self.p.x
        k = iter(range(100))
        if self.by == "x":
            h = n // 2
            a = [self.copy(next(k), "x+", x, own=True), self.copy(next(k), "x-", x, own=True), self.copy(next(k), "d", x, own=True)]
            b = [
                self.copy(next(k), "x+", x + p.nx - 1, 0, h),
                self.copy(next(k), "x-", x + 1, h, n - h),
                self.copy(next(k), "d", x + p.nx - 1),
                self.copy(next(k), "d", x + 1),
            ]
            d = [self.copy(next(k), "d", x + 2)]
            return [([], a), (a[:2], b), (b[:2], d)], a[2:] + b[2:] + d, a + b + d
        q = n // 4
        h = (q // 2 + 7) // 8 * 8
        y, yp, ym = p.y * q, ((p.y + 1) % p.ny) * q, ((p.y + p.ny - 1) % p.ny) * q
        near = (x + p.nx - 1, x + 1)
        a = [self.copy(next(k), "x+", x, y, q, own=True), self.copy(next(k), "x-", x, y, q, own=True), self.copy(next(k), "d", x, own=True)]
        b = [self.copy(next(k), "x+", near[0], y, h), self.copy(next(k), "x-", near[1], y + h, q - h)]
        b += [self.copy(next(k), way, at, y, q) for at in near for way in ("y+", "y-")]
        c = [self.copy(next(k), way, x + 2, y, q) for way in ("y+", "y-")]
        every = (*near, x + 2)
        d = [self.copy(next(k), "y+", at, ym, h) for at in every] + [self.copy(next(k), "y-", at, yp + h, q - h) for at in every]
        e = [self.copy(next(k), "d", at) for at in every]
        return [([], a), (a[:2], b), (b[:2], c), (b[2:] + c, d), (d, e)], a[2:] + e, a + b + c + d + e

    def run(self, stage):
        stages, _, _ = self.copies()
        before, now = stages[stage]
        for one in before:
            one().wait_recv()
        for one in now:
            one().start()
        if stage == 0:
            pltpu.make_async_copy(self.shard, self.stage, self.local.at[0]).start()
        if stage == 1:
            pltpu.make_async_copy(self.shard, self.stage, self.local.at[0]).wait()
            pltpu.make_async_copy(self.stage, self.full.at[self.span(self.p.x)], self.local.at[1]).start()

    def finish(self):
        _, last, every = self.copies()
        for one in last:
            one().wait_recv()
        for one in every:
            one().wait_send()
        pltpu.make_async_copy(self.stage, self.full.at[self.span(self.p.x)], self.local.at[1]).wait()


def call(mesh, name, body, steps, args, in_specs, out_specs, out_shape, flops, gathers=(), plan=(), end=(), cid=None):
    n_in, n_out, n_g = len(args), len(out_specs), len(gathers)
    group = mesh.shape["s"]

    def kernel(*refs):
        ins, refs = refs[:n_in], refs[n_in:]
        shards, refs = refs[:n_g], refs[n_g:]
        outs, refs = refs[:n_out], refs[n_out:]
        fulls, refs = refs[:n_g], refs[n_g:]
        step = pl.program_id(0)
        if n_g:
            place = Place(mesh)
            items = [
                Gather(place, by, shard.at[layer], full, *refs[4 * i : 4 * i + 4])
                for i, ((_, layer, by), shard, full) in enumerate(zip(gathers, shards, fulls, strict=True))
            ]
            for at, todo in enumerate(plan):
                if todo:

                    @pl.when(step == at)
                    def _(at=at, todo=todo):
                        if at == 0:
                            place.meet()
                        for g, stage in todo:
                            items[g].run(stage)

        body(*ins, *outs)
        if n_g:

            @pl.when(step == steps - 1)
            def _():
                for g, stage in end:
                    items[g].run(stage)
                for item in items:
                    item.finish()

    hbm = pl.BlockSpec(memory_space=pltpu.HBM)
    scratch, fulls = [], []
    for shards, _, _ in gathers:
        _, n, columns = shards.shape
        fulls.append(sds((group * n, columns)))
        scratch += [pltpu.VMEM((n, columns), BF), pltpu.SemaphoreType.DMA((20,)), pltpu.SemaphoreType.DMA((20,)), pltpu.SemaphoreType.DMA((2,))]
    nbytes = sum(a.size * a.dtype.itemsize for a in args) + sum(o.size * jnp.dtype(o.dtype).itemsize for o in out_shape)
    return pl.pallas_call(
        kernel,
        grid=(steps,),
        in_specs=list(in_specs) + [hbm] * n_g,
        out_specs=list(out_specs) + [hbm] * n_g,
        out_shape=list(out_shape) + fulls,
        scratch_shapes=scratch,
        compiler_params=pltpu.CompilerParams(
            vmem_limit_bytes=60 * 2**20,
            dimension_semantics=("arbitrary",),
            **({"collective_id": cid, "has_side_effects": True} if n_g else {}),
        ),
        cost_estimate=pl.CostEstimate(flops=flops, bytes_accessed=nbytes, transcendentals=0),
        name=name,
    )(*args, *(g[0] for g in gathers))


def prepare(mesh, x, gathers, **kw):
    tokens, d = x.shape
    block = tokens // 4

    def body(x_ref, a_ref):
        a_ref[...] = normed(x_ref[...].astype(F32))

    return call(mesh, "prepare", body, 4, [x], [rows(block, d)], [rows(block, d)], [sds(x.shape)], x.size, gathers, **kw)


def gate_up(mesh, a, wg, wu, gathers, **kw):
    (tokens, d), f = a.shape, wg.shape[1]

    def body(a_ref, g_ref, u_ref, p_ref, go_ref, uo_ref):
        g, u = mm(a_ref[...], g_ref[...]), mm(a_ref[...], u_ref[...])
        go_ref[...], uo_ref[...] = g, u
        p_ref[...] = (g * jax.nn.sigmoid(g) * u).astype(BF)

    return call(
        mesh, "gate_up", body, f // BN, [a, wg, wu], [whole(a.shape), cols(d, BN), cols(d, BN)], [cols(tokens, BN)] * 3,
        [sds((tokens, f)), sds((tokens, f), F32), sds((tokens, f), F32)], 4 * tokens * d * f, gathers, **kw
    )


def down(mesh, h, p, wd, gathers, **kw):
    (tokens, d), f = h.shape, p.shape[1]
    block = tokens // 4

    def body(h_ref, p_ref, w_ref, ho_ref, a_ref):
        new = h_ref[...] + mm(p_ref[...], w_ref[...]).astype(BF)
        ho_ref[...] = new
        a_ref[...] = normed(new.astype(F32))

    return call(
        mesh, "down", body, 4, [h, p, wd], [rows(block, d), rows(block, f), whole(wd.shape)], [rows(block, d)] * 2,
        [sds(h.shape)] * 2, 2 * tokens * d * f, gathers, **kw
    )


def by_gate_up(by_p, g, u):
    s = jax.nn.sigmoid(g)
    silu = g * s
    return (by_p * u * (s * (1 + g * (1 - s)))).astype(BF), (by_p * silu).astype(BF), silu


def last_layer(mesh, a, dy, wg, wu, wd):
    (tokens, d), f = a.shape, wg.shape[1]

    def body(a_ref, y_ref, g_ref, u_ref, d_ref, p_ref, bg_ref, bu_ref):
        g, u = mm(a_ref[...], g_ref[...]), mm(a_ref[...], u_ref[...])
        by_p = mm(y_ref[...], d_ref[...], NT).astype(BF).astype(F32)
        bg_ref[...], bu_ref[...], silu = by_gate_up(by_p, g, u)
        p_ref[...] = (silu * u).astype(BF)

    return call(
        mesh, "last_layer", body, f // BN, [a, dy, wg, wu, wd], [whole(a.shape), whole(dy.shape), cols(d, BN), cols(d, BN), rows(BN, d)],
        [cols(tokens, BN)] * 3, [sds((tokens, f))] * 3, 6 * tokens * d * f
    )


def by_hidden(mesh, g, u, dy, wd):
    (tokens, d), f = dy.shape, wd.shape[0]

    def body(g_ref, u_ref, y_ref, d_ref, bg_ref, bu_ref):
        by_p = mm(y_ref[...], d_ref[...], NT).astype(BF).astype(F32)
        bg_ref[...], bu_ref[...], _ = by_gate_up(by_p, g_ref[...], u_ref[...])

    return call(
        mesh, "by_hidden", body, f // BN, [g, u, dy, wd], [cols(tokens, BN), cols(tokens, BN), whole(dy.shape), rows(BN, d)],
        [cols(tokens, BN)] * 2, [sds((tokens, f))] * 2, 2 * tokens * d * f
    )


def by_states(mesh, dy, h, bg, bu, wg, wu):
    (tokens, d), f = h.shape, bg.shape[1]
    block = tokens // 4

    def body(y_ref, h_ref, bg_ref, bu_ref, g_ref, u_ref, o_ref):
        by_a = (mm(bg_ref[...], g_ref[...], NT).astype(BF) + mm(bu_ref[...], u_ref[...], NT).astype(BF)).astype(F32)
        x = h_ref[...].astype(F32)
        scale = lax.rsqrt(jnp.mean(x * x, -1, keepdims=True) + 1e-6)
        along = jnp.mean(by_a * x, -1, keepdims=True)
        o_ref[...] = y_ref[...] + (by_a * scale - x * (scale * scale * scale * along)).astype(BF)

    return call(
        mesh, "by_states", body, 4, [dy, h, bg, bu, wg, wu],
        [rows(block, d), rows(block, d), rows(block, f), rows(block, f), whole(wg.shape), whole(wu.shape)],
        [rows(block, d)], [sds(h.shape)], 4 * tokens * d * f
    )[0]


def by_weight(mesh, left, right, name):
    (tokens, m), n = left.shape, right.shape[1]

    def body(l_ref, r_ref, o_ref):
        o_ref[...] = mm(l_ref[...], r_ref[...], TN).astype(BF)

    return call(mesh, name, body, m // BN, [left, right], [cols(tokens, BN), whole(right.shape)], [rows(BN, n)], [sds((m, n))], 2 * tokens * m * n)[0]


def adamw(w, m, v, g):
    m = 0.9 * m + 0.1 * g
    v = 0.95 * v + 0.05 * g * g
    step = m * lax.rsqrt(v + 1e-8) + 0.1 * w
    return (w - 0.02 * step).astype(BF), m, v


def solution(mesh):
    def summed(term):
        return lax.psum(lax.psum_scatter(term, "s", scatter_dimension=0, tiled=True), "r")

    def step(x, dy, *arrays):
        weights, m, v = (arrays[i : i + 3] for i in (0, 3, 6))
        wg, wu, wd = weights
        h0, dy = x[0], dy[0]
        a0, u0, g0 = prepare(mesh, h0, [(wu, 0, "y"), (wg, 0, "x")], plan=[[(0, 0)], [], [(0, 1), (1, 0)], []],
            end=[(0, 2), (0, 3), (1, 1), (0, 4), (1, 2)], cid=0)
        p0, zg0, zu0, d0, g1 = gate_up(mesh, a0, g0, u0, [(wd, 0, "x"), (wg, 1, "y")],
            plan=[[(1, 0)], [], [(1, 1), (0, 0)], [], [(1, 2)], [], [(1, 3)], [], [], [(0, 1), (1, 4)], []],
            end=[(0, 2)], cid=1)
        h1, a1, u1, d1 = down(mesh, h0, p0, d0, [(wu, 1, "y"), (wd, 1, "x")], plan=[[(0, 0)], [(0, 1), (1, 0)], [(0, 2)], [(0, 3)]],
            end=[(1, 1), (0, 4), (1, 2)], cid=2)
        p1, bg1, bu1 = last_layer(mesh, a1, dy, g1, u1, d1)
        terms = {}

        def term(name, left, right, then):
            terms[name], *then = lax.optimization_barrier((by_weight(mesh, left, right, name), *then))
            return then

        (a1,) = term("by_down_1", p1, dy, [a1])
        (a1, bg1) = term("by_gate_1", a1, bg1, [a1, bg1])
        bg1, bu1 = term("by_up_1", a1, bu1, [bg1, bu1])
        by_h = by_states(mesh, dy, h1, bg1, bu1, g1, u1)
        by_h, zg0 = term("by_down_0", p0, by_h, [by_h, zg0])
        bg0, bu0 = by_hidden(mesh, zg0, zu0, by_h, d0)
        (bu0,) = term("by_gate_0", a0, bg0, [bu0])
        term("by_up_0", a0, bu0, [])
        mine = [[summed(terms[f"by_{one}_{number}"]) for one in ("gate", "up", "down")] for number in range(2)]
        gradients = [jnp.stack([mine[number][i] for number in range(2)]).astype(F32) for i in range(3)]
        new = [adamw(w.astype(F32), m, v, g) for w, m, v, g in zip(weights, m, v, gradients, strict=True)]
        return tuple(one[which] for which in range(3) for one in new)

    states, cut = P(("rep", "r", "s"), None, None), P(None, "s", None)
    return jax.shard_map(
        step,
        mesh=mesh,
        in_specs=(states, states) + (cut,) * 9,
        out_specs=(P("rep", "s", None),) * 9,
        check_vma=False,
    )
```

time: 705 us -> 632 us (0.90); the launches traced: 696 us -> 631 us
  Pallas kernels: 0 us -> 368 us
  matrix products: 331 us -> 0 us
  waiting for transfers between devices: 303 us -> 231 us
  local copies, waits for them, and re-layouts: 25.4 us -> 3.33 us
    pallas_call x0 -> x12, Pallas kernels: none -> 368 us  [call(): pl.pallas_call(kernel, grid=(steps,), in_specs=list(in_specs) + [hbm] * n...]
    dot_general x15 -> x0, matrix products: 331 us -> none  [the longest x5 119 us: layer(): gate = jnp.dot(a, w['w_gate'], preferred_element_type=jnp.float32)]
    all_gather x6 -> x0, waiting for transfers between devices: 103 us -> none  [fetched(): lax.all_gather(w[number], 's', axis=0, tiled=True)]
    reduce_scatter x6, waiting for transfers between devices: 104 us -> 136 us  [summed(): lax.psum_scatter(term, 's', scatter_dimension=0, tiled=True)]
    unnamed x40 -> x18, local copies, waits for them, and re-layouts: 19.1 us -> 3.33 us
  transfers between devices with their start and end apart: 13 -> 7, of which waited for: 10 -> 5; matrix products, arithmetic and copies ran while one was open for 37% -> 0% of each run, Pallas kernels for 0% -> 26%
where the time goes in v1:
time: 632 us; the launch traced here: 631 us
  Pallas kernels  368 us (58%)
  waiting for transfers between devices  231 us (37%)
  between operations  14.3 us (2%)
  other arithmetic  14.1 us (2%)
    pallas_call x12, Pallas kernels, call(): pl.pallas_call(kernel, grid=(steps,), in_specs=list(in_specs) + [hbm] * n...  368 us
    reduce_scatter x6, waiting for transfers between devices, summed(): lax.psum_scatter(term, 's', scatter_dimension=0, tiled=True)  136 us
    psum x1, waiting for transfers between devices, summed(): lax.psum(lax.psum_scatter(term, 's', scatter_dimension=0, tiled=True), 'r')  93.4 us
    convert_element_type x2, other arithmetic, adamw(): return ((w - 0.02 * step).astype(BF), m, v)  14.1 us
  transfers between devices with their start and end apart: 7, of which 5 were waited for; matrix products, arithmetic and copies ran while one was open for 0% of the time, Pallas kernels for 26%

profile of v1, /device:TPU:97, one launch (start us, length us, event | category | flops | bytes accessed | tf_op | source)
XLA Modules:
  0.0 631.4 jit_solution(8064299381180767107)
XLA Ops:
  7.2 0.1 reduce-scatter.17.cloned.1.call-start
  7.3 46.0 %prepare.1 = (bf16[2048,1024]{1,0:T(8,128)(2,1)}, bf16[1024,2816]{1,0:T(8,128)(2,1)}, bf16[1024,2816]{1,0:T(8,128)(2,1)}) custom-call(bf16[2048,1024]{1,0:T(8,128)(2,1)} %bitcast.8, bf16[2,128,2816]{2,1,0:T(8,128)(2,1)} %refs_3_.3, bf16[2,128,2816]{2,1,0:T(8,128)(2,1)} %refs_4_.2), custom_call_target="tpu_custom_call" | custom-call | flops 2097152 | bytes 8388608 | tf_op jit(solution)/shard_map/prepare/pallas_call | solution.py:171
  53.3 46.2 %gate_up.1 = (bf16[2048,2816]{1,0:T(8,128)(2,1)}, f32[2048,2816]{1,0:T(8,128)}, f32[2048,2816]{1,0:T(8,128)}, bf16[2816,1024]{1,0:T(8,128)(2,1)}, bf16[1024,2816]{1,0:T(8,128)(2,1)}) custom-call(bf16[2048,1024]{1,0:T(8,128)(2,1)} %get-tuple-element.39.refs_0_, bf16[1024,2816]{1,0:T(8,128)(2,1)} %get-tuple-element.40.refs_1_, ...), custom_call_target="tpu_custom_call" | custom-call | flops 23622320128 | bytes 73400320 | tf_op jit(solution)/shard_map/gate_up/pallas_call | solution.py:171
  99.5 44.6 %down.1 = (bf16[2048,1024]{1,0:T(8,128)(2,1)}, bf16[2048,1024]{1,0:T(8,128)(2,1)}, bf16[1024,2816]{1,0:T(8,128)(2,1)}, bf16[2816,1024]{1,0:T(8,128)(2,1)}) custom-call(bf16[2048,1024]{1,0:T(8,128)(2,1)} %bitcast.9, bf16[2048,2816]{1,0:T(8,128)(2,1)} %get-tuple-element.42.refs_1_.refs_0_, bf16[2816,1024]{1,0:T(8,128)(2,1)} %get-tuple-element.43.refs_2_.refs_3_, ...), custom_call_target="tpu_custom_call" | custom-call | flops 11811160064 | bytes 29884416 | tf_op jit(solution)/shard_map/down/pallas_call | solution.py:171
  144.1 50.3 %last_layer.1 = (bf16[2048,2816]{1,0:T(8,128)(2,1)}, bf16[2048,2816]{1,0:T(8,128)(2,1)}, bf16[2048,2816]{1,0:T(8,128)(2,1)}) custom-call(bf16[2048,1024]{1,0:T(8,128)(2,1)} %get-tuple-element.52.refs_0_, bf16[2048,1024]{1,0:T(8,128)(2,1)} %bitcast.16, bf16[1024,2816]{1,0:T(8,128)(2,1)} %get-tuple-element.46.refs_2_.refs_4_, ...), custom_call_target="tpu_custom_call" | custom-call | flops 35433480192 | bytes 60293120 | tf_op jit(solution)/shard_map/last_layer/pallas_call | solution.py:171
  194.4 18.2 %by_down_1.1 = bf16[2816,1024]{1,0:T(8,128)(2,1)} custom-call(bf16[2048,2816]{1,0:T(8,128)(2,1)} %get-tuple-element.49.refs_0_, bf16[2048,1024]{1,0:T(8,128)(2,1)} %bitcast.17), custom_call_target="tpu_custom_call" | custom-call | flops 11811160064 | bytes 21495808 | tf_op jit(solution)/shard_map/by_down_1/pallas_call | solution.py:171
  212.6 0.1 reduce-scatter.17.cloned.1.call-update
  212.6 0.2 reduce-scatter.9.cloned.1.call-start
  212.9 18.6 %by_gate_1.1 = bf16[1024,2816]{1,0:T(8,128)(2,1)} custom-call(bf16[2048,1024]{1,0:T(8,128)(2,1)} %get-tuple-element.52.refs_0_, bf16[2048,2816]{1,0:T(8,128)(2,1)} %get-tuple-element.55.refs_1_.refs_2_), custom_call_target="tpu_custom_call" | custom-call | flops 11811160064 | bytes 21495808 | tf_op jit(solution)/shard_map/by_gate_1/pallas_call | solution.py:171
  231.5 0.1 reduce-scatter.9.cloned.1.call-update
  231.6 0.1 reduce-scatter.7.cloned.1.call-start
  231.6 18.6 %by_up_1.1 = bf16[1024,2816]{1,0:T(8,128)(2,1)} custom-call(bf16[2048,1024]{1,0:T(8,128)(2,1)} %get-tuple-element.52.refs_0_, bf16[2048,2816]{1,0:T(8,128)(2,1)} %get-tuple-element.56.refs_1_.refs_3_), custom_call_target="tpu_custom_call" | custom-call | flops 11811160064 | bytes 21495808 | tf_op jit(solution)/shard_map/by_up_1/pallas_call | solution.py:171
  250.2 34.6 %by_states.1.refs_1_.refs_2_ = bf16[2048,1024]{1,0:T(8,128)(2,1)} custom-call(bf16[2048,1024]{1,0:T(8,128)(2,1)} %bitcast.18, bf16[2048,1024]{1,0:T(8,128)(2,1)} %get-tuple-element.44.refs_1_, bf16[2048,2816]{1,0:T(8,128)(2,1)} %get-tuple-element.55.refs_1_.refs_2_, bf16[2048,2816]{1,0:T(8,128)(2,1)} %get-tuple-element.56.refs_1_.refs_3_, ...), custom_call_target="tpu_custom_call" | custom-call | flops 23622320128 | bytes 47185920 | tf_op jit(solution)/shard_map/by_states/pallas_call | solution.py:171
  284.8 18.2 %by_down_0.1 = bf16[2816,1024]{1,0:T(8,128)(2,1)} custom-call(bf16[2048,2816]{1,0:T(8,128)(2,1)} %get-tuple-element.42.refs_1_.refs_0_, bf16[2048,1024]{1,0:T(8,128)(2,1)} %by_states.1.refs_1_.refs_2_), custom_call_target="tpu_custom_call" | custom-call | flops 11811160064 | bytes 21495808 | tf_op jit(solution)/shard_map/by_down_0/pallas_call | solution.py:171
  303.0 35.8 %by_hidden.1 = (bf16[2048,2816]{1,0:T(8,128)(2,1)}, bf16[2048,2816]{1,0:T(8,128)(2,1)}) custom-call(f32[2048,2816]{1,0:T(8,128)} %get-tuple-element.58.refs_0_, f32[2048,2816]{1,0:T(8,128)} %get-tuple-element.59.refs_1_, bf16[2048,1024]{1,0:T(8,128)(2,1)} %by_states.1.refs_1_.refs_2_, bf16[2816,1024]{1,0:T(8,128)(2,1)} %get-tuple-element.43.refs_2_.refs_3_), custom_call_target="tpu_custom_call" | custom-call | flops 11811160064 | bytes 79167488 | tf_op jit(solution)/shard_map/by_hidden/pallas_call | solution.py:171
  338.8 18.6 %by_gate_0.1 = bf16[1024,2816]{1,0:T(8,128)(2,1)} custom-call(bf16[2048,1024]{1,0:T(8,128)(2,1)} %get-tuple-element.39.refs_0_, bf16[2048,2816]{1,0:T(8,128)(2,1)} %get-tuple-element.61.refs_1_), custom_call_target="tpu_custom_call" | custom-call | flops 11811160064 | bytes 21495808 | tf_op jit(solution)/shard_map/by_gate_0/pallas_call | solution.py:171
  357.4 0.1 reduce-scatter.7.cloned.1.call-update
  357.5 0.1 reduce-scatter.15.cloned.1.call-start
  357.6 0.6 reduce-scatter.15.cloned.1.call-update
  358.1 0.1 reduce-scatter.13.cloned.1.call-start
  358.2 0.6 reduce-scatter.13.cloned.1.call-update
  358.8 0.3 reduce-scatter.11.cloned.1.call-start
  359.1 18.6 %by_up_0.1 = bf16[1024,2816]{1,0:T(8,128)(2,1)} custom-call(bf16[2048,1024]{1,0:T(8,128)(2,1)} %get-tuple-element.39.refs_0_, bf16[2048,2816]{1,0:T(8,128)(2,1)} %get-tuple-element.65.refs_1_), custom_call_target="tpu_custom_call" | custom-call | flops 11811160064 | bytes 21495808 | tf_op jit(solution)/shard_map/by_up_0/pallas_call | solution.py:171
  377.7 0.1 reduce-scatter.11.cloned.1.call-update
  377.7 0.0 copy-start.2
  377.7 0.1 all-reduce.3.cloned.1.call-start
  377.8 0.0 reduce-scatter.17.cloned.1.call-done
  377.8 0.0 reduce-scatter.9.cloned.1.call-done
  377.9 14.8 %reduce-scatter.7.cloned.1.call-done = bf16[128,2816]{1,0:T(8,128)(2,1)} async-done(((bf16[1024,2816]{1,0:T(8,128)(2,1)}), bf16[128,2816]{1,0:T(8,128)(2,1)}) %reduce-scatter.7.cloned.1.call-update) | async-done | bytes 720912 | tf_op jit(solution)/shard_map/reduce_scatter | solution.py:297
  392.6 40.3 %reduce-scatter.15.cloned.1.call-done = bf16[352,1024]{1,0:T(8,128)(2,1)} async-done(((bf16[2816,1024]{1,0:T(8,128)(2,1)}), bf16[352,1024]{1,0:T(8,128)(2,1)}) %reduce-scatter.15.cloned.1.call-update) | async-done | bytes 720912 | tf_op jit(solution)/shard_map/reduce_scatter | solution.py:297
  433.0 40.3 %reduce-scatter.13.cloned.1.call-done = bf16[128,2816]{1,0:T(8,128)(2,1)} async-done(((bf16[1024,2816]{1,0:T(8,128)(2,1)}), bf16[128,2816]{1,0:T(8,128)(2,1)}) %reduce-scatter.13.cloned.1.call-update) | async-done | bytes 720912 | tf_op jit(solution)/shard_map/reduce_scatter | solution.py:297
  473.3 40.3 %reduce-scatter.11.cloned.1.call-done = bf16[128,2816]{1,0:T(8,128)(2,1)} async-done(((bf16[1024,2816]{1,0:T(8,128)(2,1)}), bf16[128,2816]{1,0:T(8,128)(2,1)}) %reduce-scatter.11.cloned.1.call-update) | async-done | bytes 720912 | tf_op jit(solution)/shard_map/reduce_scatter | solution.py:297
  513.6 0.1 all-reduce.3.cloned.1.call-update
  513.6 93.4 %all-reduce.3.cloned.1.call-done = (bf16[1,128,2816]{2,1,0:T(8,128)(2,1)}, bf16[1,128,2816]{2,1,0:T(8,128)(2,1)}, bf16[1,128,2816]{2,1,0:T(8,128)(2,1)}, bf16[1,...) async-done(((bf16[1,128,2816]{2,1,0:T(8,128)(2,1)}, bf16[1,128,2816]{2,1,0:T(8,128)(2,1)}, bf16[1,128,2816]{2,1,0:T(8,128)(2,1)}, ...) | async-done | bytes 4325392 | tf_op jit(solution)/shard_map/psum | solution.py:297
  607.0 0.0 copy-done.2
  607.0 0.0 copy-start
  607.0 0.0 copy-start.1
  607.0 0.0 copy-start.3
  607.0 0.0 copy-start.4
  607.0 0.0 copy-start.5
  607.0 0.0 copy-start.6
  607.1 0.0 copy-start.7
  607.1 0.0 copy-start.8
  607.1 6.4 %fusion.10 = (bf16[2,352,1024]{2,1,0:T(8,128)(2,1)}, f32[2,352,1024]{2,1,0:T(8,128)}, f32[2,352,1024]{2,1,0:T(8,128)}) fusion(bf16[2,352,1024]{2,1,0:T(8,128)(2,1)} %refs_4_.3, bf16[1,352,1024]{2,1,0:T(8,128)(2,1)} %get-tuple-element.73, bf16[1,352,1024]{2,1,0:T(8,128)(2,1)} %get-tuple-element.74, f32[2,352,1024]{2,1,0:T(8,128)S(1)} %copy-done.2, ...), kind=kLoop, calls=%fused_computation.22 | loop fusion | flops 13697024 | bytes 15859712 | tf_op jit(solution)/shard_map/convert_element_type | solution.py:292
  613.4 0.0 copy-done
  613.4 0.0 copy-done.1
  613.5 0.0 copy-done.3
  613.5 1.4 copy-done.4
  614.8 0.8 copy-done.5
  615.6 0.8 copy-done.6
  616.5 0.1 copy-done.7
  616.6 0.2 copy-done.8
  616.8 7.8 %fusion.2 = (bf16[2,128,2816]{2,1,0:T(8,128)(2,1)}, f32[2,128,2816]{2,1,0:T(8,128)}, f32[2,128,2816]{2,1,0:T(8,128)}, bf16[2,128,2816]{2,1,0:T(8,128)(2,1)}, f32...) fusion(bf16[2,128,2816]{2,1,0:T(8,128)(2,1)S(1)} %copy-done, bf16[1,128,2816]{2,1,0:T(8,128)(2,1)S(1)} %copy-done.7, ...), kind=kLoop, calls=%fused_computation.14 | loop fusion | flops 27394048 | bytes 31719424 | tf_op jit(solution)/shard_map/convert_element_type | solution.py:292
Async XLA Ops:
  7.2 370.7 %reduce-scatter.17.cloned.1.call-start = ((), (), s32[]{:S(2)}) async-start(), calls=%async_computation.11 | async-start | bytes 6488064 | tf_op jit(solution)/shard_map/reduce_scatter | solution.py:297
  212.6 165.2 %reduce-scatter.9.cloned.1.call-start = ((), (), s32[]{:S(2)}) async-start(), calls=%async_computation.7 | async-start | bytes 6488064 | tf_op jit(solution)/shard_map/reduce_scatter | solution.py:297
  231.6 161.1 %reduce-scatter.7.cloned.1.call-start = ((), (), s32[]{:S(2)}) async-start(), calls=%async_computation.6 | async-start | bytes 6488064 | tf_op jit(solution)/shard_map/reduce_scatter | solution.py:297
  357.5 75.5 %reduce-scatter.15.cloned.1.call-start = ((), (), s32[]{:S(2)}) async-start(), calls=%async_computation.10 | async-start | bytes 6488064 | tf_op jit(solution)/shard_map/reduce_scatter | solution.py:297
  358.1 115.1 %reduce-scatter.13.cloned.1.call-start = ((), (), s32[]{:S(2)}) async-start(), calls=%async_computation.9 | async-start | bytes 6488064 | tf_op jit(solution)/shard_map/reduce_scatter | solution.py:297
  358.8 154.8 %reduce-scatter.11.cloned.1.call-start = ((), (), s32[]{:S(2)}) async-start(), calls=%async_computation.8 | async-start | bytes 6488064 | tf_op jit(solution)/shard_map/reduce_scatter | solution.py:297
  377.7 229.3 %copy-start.2 = (f32[2,352,1024]{2,1,0:T(8,128)S(1)}, f32[2,352,1024]{2,1,0:T(8,128)}, u32[]{:S(2)}) copy-start(f32[2,352,1024]{2,1,0:T(8,128)} %param.21) | copy-start | bytes 8650756
  377.7 229.3 %all-reduce.3.cloned.1.call-start = ((), (), s32[]{:S(2)}) async-start(), calls=%async_computation.12 | async-start | bytes 8650752 | tf_op jit(solution)/shard_map/psum | solution.py:297
  607.0 6.4 %copy-start = (bf16[2,128,2816]{2,1,0:T(8,128)(2,1)S(1)}, bf16[2,128,2816]{2,1,0:T(8,128)(2,1)}, u32[]{:S(2)}) copy-start(bf16[2,128,2816]{2,1,0:T(8,128)(2,1)} %refs_4_.2) | copy-start | bytes 4325380
  607.0 6.4 %copy-start.1 = (bf16[2,128,2816]{2,1,0:T(8,128)(2,1)S(1)}, bf16[2,128,2816]{2,1,0:T(8,128)(2,1)}, u32[]{:S(2)}) copy-start(bf16[2,128,2816]{2,1,0:T(8,128)(2,1)} %refs_3_.3) | copy-start | bytes 4325380
  607.0 6.4 %copy-start.3 = (f32[2,128,2816]{2,1,0:T(8,128)S(1)}, f32[2,128,2816]{2,1,0:T(8,128)}, u32[]{:S(2)}) copy-start(f32[2,128,2816]{2,1,0:T(8,128)} %param.19) | copy-start | bytes 8650756
  607.0 7.8 %copy-start.4 = (f32[2,128,2816]{2,1,0:T(8,128)S(1)}, f32[2,128,2816]{2,1,0:T(8,128)}, u32[]{:S(2)}) copy-start(f32[2,128,2816]{2,1,0:T(8,128)} %param.16) | copy-start | bytes 8650756
  607.0 8.6 %copy-start.5 = (f32[2,128,2816]{2,1,0:T(8,128)S(1)}, f32[2,128,2816]{2,1,0:T(8,128)}, u32[]{:S(2)}) copy-start(f32[2,128,2816]{2,1,0:T(8,128)} %param.20) | copy-start | bytes 8650756
  607.0 9.4 %copy-start.6 = (f32[2,128,2816]{2,1,0:T(8,128)S(1)}, f32[2,128,2816]{2,1,0:T(8,128)}, u32[]{:S(2)}) copy-start(f32[2,128,2816]{2,1,0:T(8,128)} %param.17) | copy-start | bytes 8650756
  607.1 9.5 %copy-start.7 = (bf16[1,128,2816]{2,1,0:T(8,128)(2,1)S(1)}, bf16[1,128,2816]{2,1,0:T(8,128)(2,1)}, u32[]{:S(2)}) copy-start(bf16[1,128,2816]{2,1,0:T(8,128)(2,1)} %get-tuple-element.69) | copy-start | bytes 2162692
  607.1 9.7 %copy-start.8 = (bf16[1,128,2816]{2,1,0:T(8,128)(2,1)S(1)}, bf16[1,128,2816]{2,1,0:T(8,128)(2,1)}, u32[]{:S(2)}) copy-start(bf16[1,128,2816]{2,1,0:T(8,128)(2,1)} %get-tuple-element.70) | copy-start | bytes 2162692
Sparse Core Ops, SparseCore 0:
  212.8 34.9 reduce-scatter.16
  250.1 38.0 reduce-scatter.8
  357.6 34.9 reduce-scatter.6
  394.8 38.0 reduce-scatter.14
  435.1 38.0 reduce-scatter.12
  475.4 38.0 reduce-scatter.10
  516.4 90.5 all-reduce.2

commit v2 on v1

--- a/solution.py
+++ b/solution.py
@@ -61,7 +61,6 @@
         self.p, self.by, self.shard, self.full, self.stage = place, by, shard, full, stage
         self.send, self.recv, self.local = send, recv, local
         self.n = shard.shape[0]
-        self.stages = 3 if by == "x" else 5
 
     def span(self, x, start=0, size=None):
         p = self.p
@@ -80,16 +79,13 @@
         p, n, x = self.p, self.n, self.p.x
         k = iter(range(100))
         if self.by == "x":
-            h = n // 2
-            a = [self.copy(next(k), "x+", x, own=True), self.copy(next(k), "x-", x, own=True), self.copy(next(k), "d", x, own=True)]
-            b = [
-                self.copy(next(k), "x+", x + p.nx - 1, 0, h),
-                self.copy(next(k), "x-", x + 1, h, n - h),
-                self.copy(next(k), "d", x + p.nx - 1),
-                self.copy(next(k), "d", x + 1),
-            ]
-            d = [self.copy(next(k), "d", x + 2)]
-            return [([], a), (a[:2], b), (b[:2], d)], a[2:] + b[2:] + d, a + b + d
+            h, west, east = n // 2, x + p.nx - 1, x + 1
+            a = [self.copy(next(k), "x+", x, 0, h, own=True), self.copy(next(k), "x-", x, h, n - h, own=True), self.copy(next(k), "d", x, own=True)]
+            b = [self.copy(next(k), "x+", x, h, n - h, own=True), self.copy(next(k), "x-", x, 0, h, own=True)]
+            c = [self.copy(next(k), "x+", west, 0, h), self.copy(next(k), "x-", east, h, n - h)]
+            d = [self.copy(next(k), "d", west), self.copy(next(k), "d", east)]
+            e = [self.copy(next(k), "d", x + 2)]
+            return [([], a), ([], b), (a[:2], c), (b, d), (c, e)], a[2:] + d + e, a + b + c + d + e
         q = n // 4
         h = (q // 2 + 7) // 8 * 8
         y, yp, ym = p.y * q, ((p.y + 1) % p.ny) * q, ((p.y + p.ny - 1) % p.ny) * q
@@ -125,22 +121,78 @@
         pltpu.make_async_copy(self.stage, self.full.at[self.span(self.p.x)], self.local.at[1]).wait()
 
 
-def call(mesh, name, body, steps, args, in_specs, out_specs, out_shape, flops, gathers=(), plan=(), end=(), cid=None):
-    n_in, n_out, n_g = len(args), len(out_specs), len(gathers)
-    group = mesh.shape["s"]
+class Exchange:
+    def __init__(self, place, send, recv):
+        self.p, self.send, self.recv = place, send, recv
+
+    def copy(self, k, way, src, dst):
+        return lambda: pltpu.make_async_remote_copy(
+            src_ref=src, dst_ref=dst, send_sem=self.send.at[k], recv_sem=self.recv.at[k], device_id=self.p.to[way], device_id_type=MESH
+        )
+
+    def run(self, stage):
+        before, now = self.stages[stage]
+        for one in before:
+            one().wait_recv()
+        for one in now:
+            one().start()
+
+    def finish(self):
+        waited = [one for before, _ in self.stages for one in before]
+        every = [one for _, now in self.stages for one in now]
+        for one in every:
+            if one not in waited:
+                one().wait_recv()
+        for one in every:
+            one().wait_send()
+
+
+class Beside(Exchange):
+    def __init__(self, place, mine, theirs, send, recv):
+        super().__init__(place, send, recv)
+        h = mine.shape[0] // 2
+        top, bottom = pl.ds(0, h), pl.ds(h, mine.shape[0] - h)
+        a = [self.copy(0, "y+", mine, theirs.at[0]), self.copy(1, "y-", mine, theirs.at[1])]
+        b = [self.copy(2, "y+", theirs.at[0, top], theirs.at[2, top]), self.copy(3, "y-", theirs.at[1, bottom], theirs.at[2, bottom])]
+        self.stages = [([], a), (a, b)]
+
+
+def sems(n):
+    return [pltpu.SemaphoreType.DMA((n,)), pltpu.SemaphoreType.DMA((n,))]
+
+
+def gather(mesh, shards, layer, by):
+    _, n, columns = shards.shape
+    scratch = [pltpu.VMEM((n, columns), BF), *sems(20), pltpu.SemaphoreType.DMA((2,))]
+    make = lambda place, ins, outs, scr: Gather(place, by, ins[0].at[layer], outs[0], *scr)
+    return shards, [sds((mesh.shape["s"] * n, columns))], scratch, make
+
+
+def beside(mine):
+    return mine, [sds((3, *mine.shape))], sems(4), lambda place, ins, outs, scr: Beside(place, *ins, *outs, *scr)
+
+
+def split(refs, sizes):
+    out, at = [], 0
+    for size in sizes:
+        out.append(refs[at : at + size])
+        at += size
+    return out
+
+
+def call(mesh, name, body, steps, args, in_specs, out_specs, out_shape, flops, items=(), plan=(), end=(), cid=None):
+    n_in, n_out, n_i = len(args), len(out_specs), len(items)
+    extra = [out for item in items for out in item[1]]
+    scratch = [one for item in items for one in item[2]]
 
     def kernel(*refs):
-        ins, refs = refs[:n_in], refs[n_in:]
-        shards, refs = refs[:n_g], refs[n_g:]
-        outs, refs = refs[:n_out], refs[n_out:]
-        fulls, refs = refs[:n_g], refs[n_g:]
+        ins, sources, outs, dests, scr = split(refs, [n_in, n_i, n_out, len(extra), len(scratch)])
         step = pl.program_id(0)
-        if n_g:
+        made = []
+        if n_i:
             place = Place(mesh)
-            items = [
-                Gather(place, by, shard.at[layer], full, *refs[4 * i : 4 * i + 4])
-                for i, ((_, layer, by), shard, full) in enumerate(zip(gathers, shards, fulls, strict=True))
-            ]
+            parts = zip(items, sources, split(dests, [len(i[1]) for i in items]), split(scr, [len(i[2]) for i in items]), strict=True)
+            made = [item[3](place, [source], dest, own) for item, source, dest, own in parts]
             for at, todo in enumerate(plan):
                 if todo:
 
@@ -148,54 +200,49 @@
                     def _(at=at, todo=todo):
                         if at == 0:
                             place.meet()
-                        for g, stage in todo:
-                            items[g].run(stage)
+                        for i, stage in todo:
+                            made[i].run(stage)
 
         body(*ins, *outs)
-        if n_g:
+        if n_i:
 
             @pl.when(step == steps - 1)
             def _():
-                for g, stage in end:
-                    items[g].run(stage)
-                for item in items:
-                    item.finish()
+                for i, stage in end:
+                    made[i].run(stage)
+                for one in made:
+                    one.finish()
 
     hbm = pl.BlockSpec(memory_space=pltpu.HBM)
-    scratch, fulls = [], []
-    for shards, _, _ in gathers:
-        _, n, columns = shards.shape
-        fulls.append(sds((group * n, columns)))
-        scratch += [pltpu.VMEM((n, columns), BF), pltpu.SemaphoreType.DMA((20,)), pltpu.SemaphoreType.DMA((20,)), pltpu.SemaphoreType.DMA((2,))]
     nbytes = sum(a.size * a.dtype.itemsize for a in args) + sum(o.size * jnp.dtype(o.dtype).itemsize for o in out_shape)
     return pl.pallas_call(
         kernel,
         grid=(steps,),
-        in_specs=list(in_specs) + [hbm] * n_g,
-        out_specs=list(out_specs) + [hbm] * n_g,
-        out_shape=list(out_shape) + fulls,
+        in_specs=list(in_specs) + [hbm] * n_i,
+        out_specs=list(out_specs) + [hbm] * len(extra),
+        out_shape=list(out_shape) + extra,
         scratch_shapes=scratch,
         compiler_params=pltpu.CompilerParams(
             vmem_limit_bytes=60 * 2**20,
             dimension_semantics=("arbitrary",),
-            **({"collective_id": cid, "has_side_effects": True} if n_g else {}),
+            **({"collective_id": cid, "has_side_effects": True} if n_i else {}),
         ),
         cost_estimate=pl.CostEstimate(flops=flops, bytes_accessed=nbytes, transcendentals=0),
         name=name,
-    )(*args, *(g[0] for g in gathers))
-
-
-def prepare(mesh, x, gathers, **kw):
+    )(*args, *(item[0] for item in items))
+
+
+def prepare(mesh, x, items=(), **kw):
     tokens, d = x.shape
     block = tokens // 4
 
     def body(x_ref, a_ref):
         a_ref[...] = normed(x_ref[...].astype(F32))
 
-    return call(mesh, "prepare", body, 4, [x], [rows(block, d)], [rows(block, d)], [sds(x.shape)], x.size, gathers, **kw)
-
-
-def gate_up(mesh, a, wg, wu, gathers, **kw):
+    return call(mesh, "prepare", body, 4, [x], [rows(block, d)], [rows(block, d)], [sds(x.shape)], x.size, items, **kw)
+
+
+def gate_up(mesh, a, wg, wu, items=(), **kw):
     (tokens, d), f = a.shape, wg.shape[1]
 
     def body(a_ref, g_ref, u_ref, p_ref, go_ref, uo_ref):
@@ -205,11 +252,11 @@
 
     return call(
         mesh, "gate_up", body, f // BN, [a, wg, wu], [whole(a.shape), cols(d, BN), cols(d, BN)], [cols(tokens, BN)] * 3,
-        [sds((tokens, f)), sds((tokens, f), F32), sds((tokens, f), F32)], 4 * tokens * d * f, gathers, **kw
+        [sds((tokens, f)), sds((tokens, f), F32), sds((tokens, f), F32)], 4 * tokens * d * f, items, **kw
     )
 
 
-def down(mesh, h, p, wd, gathers, **kw):
+def down(mesh, h, p, wd, items=(), **kw):
     (tokens, d), f = h.shape, p.shape[1]
     block = tokens // 4
 
@@ -220,7 +267,7 @@
 
     return call(
         mesh, "down", body, 4, [h, p, wd], [rows(block, d), rows(block, f), whole(wd.shape)], [rows(block, d)] * 2,
-        [sds(h.shape)] * 2, 2 * tokens * d * f, gathers, **kw
+        [sds(h.shape)] * 2, 2 * tokens * d * f, items, **kw
     )
 
 
@@ -245,7 +292,7 @@
     )
 
 
-def by_hidden(mesh, g, u, dy, wd):
+def by_hidden(mesh, g, u, dy, wd, items=(), **kw):
     (tokens, d), f = dy.shape, wd.shape[0]
 
     def body(g_ref, u_ref, y_ref, d_ref, bg_ref, bu_ref):
@@ -254,11 +301,11 @@
 
     return call(
         mesh, "by_hidden", body, f // BN, [g, u, dy, wd], [cols(tokens, BN), cols(tokens, BN), whole(dy.shape), rows(BN, d)],
-        [cols(tokens, BN)] * 2, [sds((tokens, f))] * 2, 2 * tokens * d * f
+        [cols(tokens, BN)] * 2, [sds((tokens, f))] * 2, 2 * tokens * d * f, items, **kw
     )
 
 
-def by_states(mesh, dy, h, bg, bu, wg, wu):
+def by_states(mesh, dy, h, bg, bu, wg, wu, items=(), **kw):
     (tokens, d), f = h.shape, bg.shape[1]
     block = tokens // 4
 
@@ -272,17 +319,212 @@
     return call(
         mesh, "by_states", body, 4, [dy, h, bg, bu, wg, wu],
         [rows(block, d), rows(block, d), rows(block, f), rows(block, f), whole(wg.shape), whole(wu.shape)],
-        [rows(block, d)], [sds(h.shape)], 4 * tokens * d * f
-    )[0]
-
-
-def by_weight(mesh, left, right, name):
+        [rows(block, d)], [sds(h.shape)], 4 * tokens * d * f, items, **kw
+    )
+
+
+def by_weight(mesh, left, right, name, items=(), **kw):
     (tokens, m), n = left.shape, right.shape[1]
 
     def body(l_ref, r_ref, o_ref):
         o_ref[...] = mm(l_ref[...], r_ref[...], TN).astype(BF)
 
-    return call(mesh, name, body, m // BN, [left, right], [cols(tokens, BN), whole(right.shape)], [rows(BN, n)], [sds((m, n))], 2 * tokens * m * n)[0]
+    return call(mesh, name, body, m // BN, [left, right], [cols(tokens, BN), whole(right.shape)], [rows(BN, n)], [sds((m, n))], 2 * tokens * m * n, items, **kw)
+
+
+def by_weights(mesh, lefts, rights, cid):
+    (tokens, m), n, many = lefts[0].shape, rights[0].shape[1], len(rights)
+    nx, ny = mesh.shape["s"] // 2, mesh.shape["r"]
+    block, own = m // nx, m // (2 * nx)
+    half, steps = own // 2, many * nx
+    part = own // ny
+    piece = part // 2
+    away = (2, 1, nx - 1, 0)
+
+    def kernel(l0_ref, l1_ref, r0_hbm, r1_hbm, r2_hbm, o_ref, rhs_ref, t_ref, r_ref, h_ref, x_ref, y_ref, a_ref, b_ref, g_ref, s_sem, send, recv):
+        step = pl.program_id(0)
+        place = Place(mesh)
+        mine = pl.ds(pl.multiple_of(place.c * own, 8), own)
+        other = pl.ds(pl.multiple_of((1 - place.c) * own, 8), own)
+        top, bottom = pl.ds(0, half), pl.ds(half, own - half)
+
+        def copy(k, way, src, dst):
+            return pltpu.make_async_remote_copy(
+                src_ref=src, dst_ref=dst, send_sem=send.at[k], recv_sem=recv.at[k], device_id=place.to[way], device_id_type=MESH
+            )
+
+        def swap(i):
+            return copy(i, "d", t_ref.at[i % 3, other], r_ref.at[i])
+
+        def far(w, up):
+            part = top if up else bottom
+            return copy(12 + 2 * w + up, "x+" if up else "x-", r_ref.at[4 * w, part], h_ref.at[w, 1 - up])
+
+        def near(w, up):
+            return copy(18 + 2 * w + up, "x+" if up else "x-", r_ref.at[4 * w + (1 if up else 2)], x_ref.at[w, 1 - up])
+
+        def at(quarter, up=None):
+            start = lax.rem(place.y + quarter, ny) * part
+            return pl.ds(pl.multiple_of(start + (piece if up == 0 else 0), 16), part if up is None else piece)
+
+        def y_far(w, up):
+            return copy(24 + 2 * w + up, "y+" if up else "y-", y_ref.at[w, at(2, up)], a_ref.at[w, 1 - up])
+
+        def y_near(w, up):
+            return copy(30 + 2 * w + up, "y+" if up else "y-", y_ref.at[w, at(1 if up else ny - 1)], b_ref.at[w, 1 - up])
+
+        def y_back(w, up):
+            return copy(36 + 2 * w + up, "y+" if up else "y-", g_ref.at[w, at(0)], g_ref.at[w, at(0)])
+
+        def y_across(w, up):
+            rows_ = at(ny - 1 if up else 1, up)
+            return copy(42 + 2 * w + up, "y+" if up else "y-", g_ref.at[w, rows_], g_ref.at[w, rows_])
+
+        def add_swapped(i):
+            swap(i).wait()
+            r_ref[i] = (r_ref[i].astype(F32) + t_ref[i % 3, mine].astype(F32)).astype(BF)
+
+        def add_far(w):
+            far(w, 1).wait_recv()
+            r_ref[4 * w + 1, top] = (r_ref[4 * w + 1, top].astype(F32) + h_ref[w, 0].astype(F32)).astype(BF)
+            far(w, 0).wait_recv()
+            r_ref[4 * w + 2, bottom] = (r_ref[4 * w + 2, bottom].astype(F32) + h_ref[w, 1].astype(F32)).astype(BF)
+
+        def start(make, w):
+            make(w, 1).start()
+            make(w, 0).start()
+
+        def add_near(w):
+            near(w, 1).wait_recv()
+            near(w, 0).wait_recv()
+            total = r_ref[4 * w + 3].astype(F32) + (x_ref[w, 0].astype(F32) + x_ref[w, 1].astype(F32))
+            y_ref[w] = total.astype(BF)
+
+        def add_y_far(w):
+            y_far(w, 1).wait()
+            y_far(w, 0).wait()
+            up, down_ = at(1, 1), at(ny - 1, 0)
+            y_ref[w, up] = (y_ref[w, up].astype(F32) + a_ref[w, 0].astype(F32)).astype(BF)
+            y_ref[w, down_] = (y_ref[w, down_].astype(F32) + a_ref[w, 1].astype(F32)).astype(BF)
+
+        def add_y_near(w):
+            y_near(w, 1).wait()
+            y_near(w, 0).wait()
+            whole_sum = y_ref[w, at(0)].astype(F32) + (b_ref[w, 0].astype(F32) + b_ref[w, 1].astype(F32))
+            g_ref[w, at(0)] = whole_sum.astype(BF)
+
+        def pass_on(w):
+            y_back(w, 1).wait()
+            y_back(w, 0).wait()
+            start(y_across, w)
+
+        def put(w):
+            y_across(w, 1).wait()
+            y_across(w, 0).wait()
+            o_ref[w] = g_ref[w]
+
+        load = [pltpu.make_async_copy(r, rhs_ref.at[w % 2], s_sem.at[w]) for w, r in enumerate((r0_hbm, r1_hbm, r2_hbm))]
+        for now in range(steps):
+
+            @pl.when(step == now)
+            def _(now=now):
+                if now == 0:
+                    load[0].start()
+                    load[1].start()
+                    place.meet()
+                    load[0].wait()
+                if now == nx:
+                    load[2].start()
+                    load[1].wait()
+                if now == 2 * nx:
+                    load[2].wait()
+                if now >= 1:
+                    swap(now - 1).start()
+                if now >= 2:
+                    add_swapped(now - 2)
+                if now == 5:
+                    add_far(0)
+                if now == 6:
+                    start(near, 0)
+                if now % nx == 3:
+                    start(far, now // nx)
+                if now == 10:
+                    add_near(0)
+                if now == 11:
+                    start(y_far, 0)
+
+        k = lax.rem(step, nx)
+        shift = jnp.where(k == 0, away[0], jnp.where(k == 1, away[1], jnp.where(k == 2, away[2], away[3])))
+        columns = pl.ds(pl.multiple_of(lax.rem(place.x + shift, nx) * block, block), block)
+        slot = lax.rem(step, 3)
+        for w, (l_ref, buffer) in enumerate(((l0_ref, 0), (l1_ref, 1), (l1_ref, 0))):
+
+            @pl.when((step >= w * nx) & (step < (w + 1) * nx))
+            def _(l_ref=l_ref, buffer=buffer):
+                t_ref[slot] = mm(l_ref[:, columns], rhs_ref[buffer], TN).astype(BF)
+
+        @pl.when(step == steps - 1)
+        def _():
+            add_swapped(10)
+            swap(11).start()
+            add_far(1)
+            add_y_far(0)
+            start(near, 1)
+            start(y_near, 0)
+            add_swapped(11)
+            add_far(2)
+            add_y_near(0)
+            start(near, 2)
+            start(y_back, 0)
+            pass_on(0)
+            add_near(1)
+            put(0)
+            start(y_far, 1)
+            add_y_far(1)
+            start(y_near, 1)
+            add_y_near(1)
+            start(y_back, 1)
+            pass_on(1)
+            add_near(2)
+            put(1)
+            start(y_far, 2)
+            add_y_far(2)
+            start(y_near, 2)
+            add_y_near(2)
+            start(y_back, 2)
+            pass_on(2)
+            put(2)
+            for w in range(many):
+                for make in (far, near):
+                    make(w, 1).wait_send()
+                    make(w, 0).wait_send()
+
+    hbm = pl.BlockSpec(memory_space=pltpu.HBM)
+    return pl.pallas_call(
+        kernel,
+        grid=(steps,),
+        in_specs=[whole(lefts[0].shape)] * 2 + [hbm] * many,
+        out_specs=whole((many, own, n)),
+        out_shape=sds((many, own, n)),
+        scratch_shapes=[
+            pltpu.VMEM((2, *rights[0].shape), BF),
+            pltpu.VMEM((3, block, n), BF),
+            pltpu.VMEM((many * nx, own, n), BF),
+            pltpu.VMEM((many, 2, half, n), BF),
+            pltpu.VMEM((many, 2, own, n), BF),
+            pltpu.VMEM((many, own, n), BF),
+            pltpu.VMEM((many, 2, piece, n), BF),
+            pltpu.VMEM((many, 2, part, n), BF),
+            pltpu.VMEM((many, own, n), BF),
+            pltpu.SemaphoreType.DMA((many,)),
+            *sems(48),
+        ],
+        compiler_params=pltpu.CompilerParams(
+            vmem_limit_bytes=63 * 2**20, dimension_semantics=("arbitrary",), collective_id=cid, has_side_effects=True
+        ),
+        cost_estimate=pl.CostEstimate(flops=12 * tokens * m * n, bytes_accessed=6 * tokens * n, transcendentals=0),
+        name="by_weights",
+    )(*lefts, *rights)
 
 
 def adamw(w, m, v, g):
@@ -300,29 +542,36 @@
         weights, m, v = (arrays[i : i + 3] for i in (0, 3, 6))
         wg, wu, wd = weights
         h0, dy = x[0], dy[0]
-        a0, u0, g0 = prepare(mesh, h0, [(wu, 0, "y"), (wg, 0, "x")], plan=[[(0, 0)], [], [(0, 1), (1, 0)], []],
-            end=[(0, 2), (0, 3), (1, 1), (0, 4), (1, 2)], cid=0)
-        p0, zg0, zu0, d0, g1 = gate_up(mesh, a0, g0, u0, [(wd, 0, "x"), (wg, 1, "y")],
-            plan=[[(1, 0)], [], [(1, 1), (0, 0)], [], [(1, 2)], [], [(1, 3)], [], [], [(0, 1), (1, 4)], []],
-            end=[(0, 2)], cid=1)
-        h1, a1, u1, d1 = down(mesh, h0, p0, d0, [(wu, 1, "y"), (wd, 1, "x")], plan=[[(0, 0)], [(0, 1), (1, 0)], [(0, 2)], [(0, 3)]],
-            end=[(1, 1), (0, 4), (1, 2)], cid=2)
+        keep = lax.optimization_barrier
+        a0, u0, g0 = prepare(mesh, h0, [gather(mesh, wu, 0, "y"), gather(mesh, wg, 0, "x")], plan=[[(0, 0), (1, 0)], [], [(0, 1), (1, 1)], []],
+            end=[(0, 2), (1, 2), (0, 3), (1, 3), (0, 4), (1, 4)], cid=0)
+        p0, zg0, zu0, d0, g1 = gate_up(mesh, a0, g0, u0, [gather(mesh, wd, 0, "x"), gather(mesh, wg, 1, "y")],
+            plan=[[(1, 0), (0, 0)], [], [(1, 1), (0, 1)], [], [(1, 2)], [(0, 2)], [], [(1, 3)], [], [(0, 3)], [(1, 4)]],
+            end=[(0, 4)], cid=1)
+        h1, a1, u1, d1 = down(mesh, h0, p0, d0, [gather(mesh, wu, 1, "y"), gather(mesh, wd, 1, "x")],
+            plan=[[(0, 0), (1, 0)], [(0, 1), (1, 1)], [(0, 2)], [(1, 2)]], end=[(0, 3), (1, 3), (0, 4), (1, 4)], cid=2)
         p1, bg1, bu1 = last_layer(mesh, a1, dy, g1, u1, d1)
-        terms = {}
-
-        def term(name, left, right, then):
-            terms[name], *then = lax.optimization_barrier((by_weight(mesh, left, right, name), *then))
-            return then
-
-        (a1,) = term("by_down_1", p1, dy, [a1])
-        (a1, bg1) = term("by_gate_1", a1, bg1, [a1, bg1])
-        bg1, bu1 = term("by_up_1", a1, bu1, [bg1, bu1])
-        by_h = by_states(mesh, dy, h1, bg1, bu1, g1, u1)
-        by_h, zg0 = term("by_down_0", p0, by_h, [by_h, zg0])
-        bg0, bu0 = by_hidden(mesh, zg0, zu0, by_h, d0)
-        (bu0,) = term("by_gate_0", a0, bg0, [bu0])
-        term("by_up_0", a0, bu0, [])
-        mine = [[summed(terms[f"by_{one}_{number}"]) for one in ("gate", "up", "down")] for number in range(2)]
+
+        def scattered(term):
+            return lax.psum_scatter(term, "s", scatter_dimension=0, tiled=True)
+
+        def total(mine, theirs):
+            mine, theirs = mine.astype(F32), theirs.astype(F32)
+            return ((mine + theirs[2]) + (theirs[0] + theirs[1])).astype(BF)
+
+        by_down, a1 = keep((*by_weight(mesh, p1, dy, "by_down_1"), a1))
+        down_1 = scattered(by_down)
+        by_gate, a1, bg1 = keep((*by_weight(mesh, a1, bg1, "by_gate_1"), a1, bg1))
+        gate_1 = scattered(by_gate)
+        (by_h,) = by_states(mesh, dy, h1, bg1, bu1, g1, u1)
+        down_1, by_h = keep((down_1, by_h))
+        by_down, by_h, zg0 = keep((*by_weight(mesh, p0, by_h, "by_down_0"), by_h, zg0))
+        down_0 = scattered(by_down)
+        bg0, bu0, down_1_y = by_hidden(mesh, zg0, zu0, by_h, d0, [beside(down_1)], plan=[[(0, 0)], [], [], [], [], [], [], [(0, 1)], [], [], []], cid=4)
+        gate_1, down_0, bg0 = keep((gate_1, down_0, bg0))
+        gate_1, down_0 = lax.psum(gate_1, "r"), lax.psum(down_0, "r")
+        three = by_weights(mesh, [a1, a0], [bu1, bg0, bu0], cid=3)
+        mine = [[three[1], three[2], down_0], [gate_1, three[0], total(down_1, down_1_y)]]
         gradients = [jnp.stack([mine[number][i] for number in range(2)]).astype(F32) for i in range(3)]
         new = [adamw(w.astype(F32), m, v, g) for w, m, v, g in zip(weights, m, v, gradients, strict=True)]
         return tuple(one[which] for which in range(3) for one in new)

time: 632 us -> 485 us (0.77)
  the two profiles are of different devices: /device:TPU:97 before, /device:TPU:98 now
where the time goes in v2:
time: 485 us; the launch traced here: 475 us
  Pallas kernels  434 us (89%)
  other arithmetic  18.3 us (4%)
  between operations  14.4 us (3%)
    pallas_call x9, Pallas kernels, call(): pl.pallas_call(kernel, grid=(steps,), in_specs=list(in_specs) + [hbm] * n...  307 us
    pallas_call x1, Pallas kernels, by_weights(): pl.pallas_call(kernel, grid=(steps,), in_specs=[whole(lefts[0].shape)] *...  127 us
    convert_element_type x3, other arithmetic, adamw(): return ((w - 0.02 * step).astype(BF), m, v)  15.6 us
  transfers between devices with their start and end apart: 4, of which 1 were waited for; matrix products, arithmetic and copies ran while one was open for 2% of the time, Pallas kernels for 50%

profile of v2, /device:TPU:98, one launch (start us, length us, event | category | flops | bytes accessed | tf_op | source)
XLA Modules:
  0.0 475.1 jit_solution(828492804666980635)
XLA Ops:
  7.2 0.1 reduce-scatter.6.cloned.1.call-start
  7.3 40.5 %prepare.1 = (bf16[2048,1024]{1,0:T(8,128)(2,1)}, bf16[1024,2816]{1,0:T(8,128)(2,1)}, bf16[1024,2816]{1,0:T(8,128)(2,1)}) custom-call(bf16[2048,1024]{1,0:T(8,128)(2,1)} %bitcast.22, bf16[2,128,2816]{2,1,0:T(8,128)(2,1)} %refs_3_.3, bf16[2,128,2816]{2,1,0:T(8,128)(2,1)} %refs_4_.2), custom_call_target="tpu_custom_call" | custom-call | flops 2097152 | bytes 8388608 | tf_op jit(solution)/shard_map/prepare/pallas_call | solution.py:218
  47.7 44.9 %gate_up.1 = (bf16[2048,2816]{1,0:T(8,128)(2,1)}, f32[2048,2816]{1,0:T(8,128)}, f32[2048,2816]{1,0:T(8,128)}, bf16[2816,1024]{1,0:T(8,128)(2,1)}, bf16[1024,2816]{1,0:T(8,128)(2,1)}) custom-call(bf16[2048,1024]{1,0:T(8,128)(2,1)} %get-tuple-element.40.refs_0_.l1_ref, bf16[1024,2816]{1,0:T(8,128)(2,1)} %get-tuple-element.41.refs_1_, ...), custom_call_target="tpu_custom_call" | custom-call | flops 23622320128 | bytes 73400320 | tf_op jit(solution)/shard_map/gate_up/pallas_call | solution.py:218
  92.6 43.6 %down.1 = (bf16[2048,1024]{1,0:T(8,128)(2,1)}, bf16[2048,1024]{1,0:T(8,128)(2,1)}, bf16[1024,2816]{1,0:T(8,128)(2,1)}, bf16[2816,1024]{1,0:T(8,128)(2,1)}) custom-call(bf16[2048,1024]{1,0:T(8,128)(2,1)} %bitcast.23, bf16[2048,2816]{1,0:T(8,128)(2,1)} %get-tuple-element.43.refs_1_.refs_0_, bf16[2816,1024]{1,0:T(8,128)(2,1)} %get-tuple-element.44.refs_2_.refs_3_, ...), custom_call_target="tpu_custom_call" | custom-call | flops 11811160064 | bytes 29884416 | tf_op jit(solution)/shard_map/down/pallas_call | solution.py:218
  136.2 50.4 %last_layer.1 = (bf16[2048,2816]{1,0:T(8,128)(2,1)}, bf16[2048,2816]{1,0:T(8,128)(2,1)}, bf16[2048,2816]{1,0:T(8,128)(2,1)}) custom-call(bf16[2048,1024]{1,0:T(8,128)(2,1)} %get-tuple-element.52.refs_0_.l0_ref, bf16[2048,1024]{1,0:T(8,128)(2,1)} %bitcast.26, bf16[1024,2816]{1,0:T(8,128)(2,1)} %get-tuple-element.46.refs_2_.refs_4_, ...), custom_call_target="tpu_custom_call" | custom-call | flops 35433480192 | bytes 60293120 | tf_op jit(solution)/shard_map/last_layer/pallas_call | solution.py:218
  186.6 18.2 %by_down_1.1 = bf16[2816,1024]{1,0:T(8,128)(2,1)} custom-call(bf16[2048,2816]{1,0:T(8,128)(2,1)} %get-tuple-element.49.refs_0_, bf16[2048,1024]{1,0:T(8,128)(2,1)} %bitcast.27), custom_call_target="tpu_custom_call" | custom-call | flops 11811160064 | bytes 21495808 | tf_op jit(solution)/shard_map/by_down_1/pallas_call | solution.py:218
  204.8 0.1 reduce-scatter.6.cloned.1.call-update
  204.9 0.2 reduce-scatter.4.cloned.1.call-start
  205.1 18.6 %by_gate_1.1 = bf16[1024,2816]{1,0:T(8,128)(2,1)} custom-call(bf16[2048,1024]{1,0:T(8,128)(2,1)} %get-tuple-element.52.refs_0_.l0_ref, bf16[2048,2816]{1,0:T(8,128)(2,1)} %get-tuple-element.57.refs_1_.refs_2_), custom_call_target="tpu_custom_call" | custom-call | flops 11811160064 | bytes 21495808 | tf_op jit(solution)/shard_map/by_gate_1/pallas_call | solution.py:218
  223.7 0.1 reduce-scatter.4.cloned.1.call-update
  223.7 0.1 reduce-scatter.8.cloned.1.call-start
  223.8 34.6 %by_states.1.refs_1_.refs_2_ = bf16[2048,1024]{1,0:T(8,128)(2,1)} custom-call(bf16[2048,1024]{1,0:T(8,128)(2,1)} %bitcast.28, bf16[2048,1024]{1,0:T(8,128)(2,1)} %get-tuple-element.56.refs_1_, bf16[2048,2816]{1,0:T(8,128)(2,1)} %get-tuple-element.57.refs_1_.refs_2_, bf16[2048,2816]{1,0:T(8,128)(2,1)} %get-tuple-element.53.refs_3_.r0_hbm, ...), custom_call_target="tpu_custom_call" | custom-call | flops 23622320128 | bytes 47185920 | tf_op jit(solution)/shard_map/by_states/pallas_call | solution.py:218
  258.4 0.0 reduce-scatter.6.cloned.1.call-done.refs_4_
  258.4 18.2 %by_down_0.1 = bf16[2816,1024]{1,0:T(8,128)(2,1)} custom-call(bf16[2048,2816]{1,0:T(8,128)(2,1)} %get-tuple-element.43.refs_1_.refs_0_, bf16[2048,1024]{1,0:T(8,128)(2,1)} %by_states.1.refs_1_.refs_2_), custom_call_target="tpu_custom_call" | custom-call | flops 11811160064 | bytes 21495808 | tf_op jit(solution)/shard_map/by_down_0/pallas_call | solution.py:218
  276.7 0.1 reduce-scatter.8.cloned.1.call-update
  276.7 0.1 all-reduce.3.cloned.1.call-start
  276.8 37.8 %by_hidden.1 = (bf16[2048,2816]{1,0:T(8,128)(2,1)}, bf16[2048,2816]{1,0:T(8,128)(2,1)}, bf16[3,352,1024]{2,1,0:T(8,128)(2,1)}) custom-call(f32[2048,2816]{1,0:T(8,128)} %get-tuple-element.61.refs_0_, f32[2048,2816]{1,0:T(8,128)} %get-tuple-element.62.refs_1_, bf16[2048,1024]{1,0:T(8,128)(2,1)} %by_states.1.refs_1_.refs_2_, ...), custom_call_target="tpu_custom_call" | custom-call | flops 11811160064 | bytes 79167488 | tf_op jit(solution)/shard_map/by_hidden/pallas_call | solution.py:218
  314.6 0.0 copy-start.2
  314.6 2.1 convert_element_type.44
  316.7 0.0 copy-done.2
  316.7 0.6 fusion.19
  317.3 0.0 reduce-scatter.4.cloned.1.call-done
  317.4 3.8 reduce-scatter.8.cloned.1.call-done
  321.2 0.1 all-reduce.3.cloned.1.call-update
  321.2 127.0 %by_weights.1 = bf16[3,128,2816]{2,1,0:T(8,128)(2,1)} custom-call(bf16[2048,1024]{1,0:T(8,128)(2,1)} %get-tuple-element.52.refs_0_.l0_ref, bf16[2048,1024]{1,0:T(8,128)(2,1)} %get-tuple-element.40.refs_0_.l1_ref, bf16[2048,2816]{1,0:T(8,128)(2,1)} %get-tuple-element.53.refs_3_.r0_hbm, bf16[2048,2816]{1,0:T(8,128)(2,1)} %get-tuple-element.66.r1_hbm, ...), custom_call_target="tpu_custom_call" | custom-call | flops 70866960384 | bytes 34603008 | tf_op jit(solution)/shard_map/by_weights/pallas_call | solution.py:503
  448.2 0.0 copy-start
  448.2 0.0 copy-start.3
  448.2 1.8 fusion.26
  450.1 0.2 copy-done
  450.2 0.9 copy-done.3
  451.1 5.1 %fusion.6 = (bf16[2,128,2816]{2,1,0:T(8,128)(2,1)}, f32[2,128,2816]{2,1,0:T(8,128)}, f32[2,128,2816]{2,1,0:T(8,128)}) fusion(bf16[2,128,2816]{2,1,0:T(8,128)(2,1)S(1)} %copy-done, bf16[1,128,2816]{2,1,0:T(8,128)(2,1)S(1)} %get-tuple-element.83, bf16[1,128,2816]{2,1,0:T(8,128)(2,1)S(1)} %get-tuple-element.82, f32[2,128,2816]{2,1,0:T(8,128)S(1)} %copy-done.3, ...), kind=kLoop, calls=%fused_computation.18 | loop fusion | flops 13697024 | bytes 15859712 | tf_op jit(solution)/shard_map/convert_element_type | solution.py:534
  456.2 0.0 all-reduce.3.cloned.1.call-done
  456.2 0.0 copy-start.1
  456.2 0.0 copy-start.4
  456.2 0.0 copy-start.5
  456.3 0.0 copy-start.6
  456.3 6.7 %fusion.10 = (bf16[2,352,1024]{2,1,0:T(8,128)(2,1)}, f32[2,352,1024]{2,1,0:T(8,128)}, f32[2,352,1024]{2,1,0:T(8,128)}) fusion(bf16[2,352,1024]{2,1,0:T(8,128)(2,1)} %refs_4_.3, bf16[1,352,1024]{2,1,0:T(8,128)(2,1)S(1)} %fusion.19, bf16[1,352,1024]{2,1,0:T(8,128)(2,1)} %get-tuple-element.72, f32[2,352,1024]{2,1,0:T(8,128)} %param.21, f32[2,352,1024]{2,1,0:T(8,128)} %param.18), kind=kLoop, calls=%fused_computation.22 | loop fusion | flops 13697024 | bytes 15859712 | tf_op jit(solution)/shard_map/convert_element_type | solution.py:534
  463.0 0.0 copy-done.1
  463.0 0.0 copy-done.4
  463.0 1.3 copy-done.5
  464.3 0.1 copy-done.6
  464.4 3.7 fusion.2
Async XLA Ops:
  7.2 251.2 %reduce-scatter.6.cloned.1.call-start = ((), (), s32[]{:S(2)}) async-start(), calls=%async_computation.4 | async-start | bytes 6488064 | tf_op jit(solution)/shard_map/reduce_scatter | solution.py:556
  204.9 112.5 %reduce-scatter.4.cloned.1.call-start = ((), (), s32[]{:S(2)}) async-start(), calls=%async_computation.3 | async-start | bytes 6488064 | tf_op jit(solution)/shard_map/reduce_scatter | solution.py:556
  223.7 97.4 %reduce-scatter.8.cloned.1.call-start = ((), (), s32[]{:S(2)}) async-start(), calls=%async_computation.5 | async-start | bytes 6488064 | tf_op jit(solution)/shard_map/reduce_scatter | solution.py:556
  276.7 179.5 %all-reduce.3.cloned.1.call-start = ((), (), s32[]{:S(2)}) async-start(), calls=%async_computation.6 | async-start | bytes 2883584 | tf_op jit(solution)/shard_map/psum | solution.py:572
  314.6 2.1 copy-start.2
  448.2 2.0 copy-start
  448.2 2.9 copy-start.3
  456.2 6.8 %copy-start.1 = (bf16[2,128,2816]{2,1,0:T(8,128)(2,1)S(1)}, bf16[2,128,2816]{2,1,0:T(8,128)(2,1)}, u32[]{:S(2)}) copy-start(bf16[2,128,2816]{2,1,0:T(8,128)(2,1)} %refs_4_.2) | copy-start | bytes 4325380
  456.2 6.8 %copy-start.4 = (f32[2,128,2816]{2,1,0:T(8,128)S(1)}, f32[2,128,2816]{2,1,0:T(8,128)}, u32[]{:S(2)}) copy-start(f32[2,128,2816]{2,1,0:T(8,128)} %param.19) | copy-start | bytes 8650756
  456.2 8.0 %copy-start.5 = (f32[2,128,2816]{2,1,0:T(8,128)S(1)}, f32[2,128,2816]{2,1,0:T(8,128)}, u32[]{:S(2)}) copy-start(f32[2,128,2816]{2,1,0:T(8,128)} %param.16) | copy-start | bytes 8650756
  456.3 8.1 %copy-start.6 = (bf16[1,128,2816]{2,1,0:T(8,128)(2,1)S(1)}, bf16[1,128,2816]{2,1,0:T(8,128)(2,1)}, u32[]{:S(2)}) copy-start(bf16[1,128,2816]{2,1,0:T(8,128)(2,1)} %get-tuple-element.71) | copy-start | bytes 2162692
Sparse Core Ops, SparseCore 0:
  205.0 35.1 reduce-scatter.5
  242.5 38.1 reduce-scatter.3
  283.0 38.1 reduce-scatter.7
  323.5 46.3 all-reduce.2
